TPU v7x, 32 devices: a whole 2x2x4 slice. The times are simulated.
32 devices in a mesh: vx: 4 (over y, x), vy: 8 (over z, core).
Axes of the slice: x: 2, y: 2, z: 4, core: 2. Of those that a mesh axis runs over, the one named last changes fastest.
Arguments:
- tokens: bfloat16 [96, 1, 256, 1024], P(('vx', 'vy')), may hold values from -256 to 256
- var_embed: bfloat16 [91, 1024], replicated, may hold values from -2 to 2
- query: bfloat16 [1024], replicated, may hold values from -6 to 6
- key_weight: bfloat16 [1024, 1024], P('vy'), may hold values from -1 to 1
- value_weight: bfloat16 [1024, 1024], P('vy'), may hold values from -0.1875 to 0.1875
- out_weight: bfloat16 [1024, 1024], P('vy'), may hold values from -0.1875 to 0.1875
- var_slot: int32 [91], replicated, may hold values from 0 to 95, as said below
Outputs:
- aggregated: bfloat16 [1, 256, 1024], P(None, ('vx', 'vy'))
Inputs may be any that keep to these rules, and one draw needn't show every extreme that they name: `var_slot`: distinct slot numbers; at least one device's slot holds a variable.
All inputs are finite; a program needn't handle non-finite values.
Results may differ from a plain program's by a relative error of at most 0.0096.
Values may be sent and summed in bfloat16 or wider, within the bound.
A program may use at most 64 MiB of HBM per device.

v0:
```python
import functools
import math

import jax
import jax.numpy as jnp
from jax import lax
from jax.experimental import pallas as pl
from jax.experimental.pallas import tpu as pltpu
from jax.sharding import PartitionSpec as P

HEADS = 16
CORES = 2
LOWEST = -1e38
F32 = jnp.float32
BF16 = jnp.bfloat16
MESH = pl.DeviceIdType.MESH
NT = (((1,), (1,)), ((), ()))


def split(x):
    high = x.astype(BF16)
    return high, (x - high.astype(F32)).astype(BF16)


def dot(a, b):
    return jnp.dot(a, b, preferred_element_type=F32)


def kernel(nx, ny, heads, tok_any, emb_any, qry_any, wk_any, wv_any, wo_any, slot_any, out,
           tok, emb, qry, wk, wo, slot, load_s,
           mixed, wbuf, kq_mine, kq_in, kq_all, ex, stat, st_in, st2, st2_in, fexp,
           part, in1, p2, in2, o3, in3,
           kq_s, kq_r, w_s, w_r, wp_s, wp_r, st_s, st_r, st2_s, st2_r, s1_s, s1_r, s2_s, s2_r, s3_s, s3_r):
    slots, patches, width = tok.shape
    rows = width // ny
    na = ny // CORES
    group = patches // nx
    piece = rows // nx
    wide = CORES * rows
    own = patches // (nx * ny)
    hdim = width // heads
    scale = 1.0 / math.sqrt(hdim)
    i = lax.axis_index("vx")
    j = lax.axis_index("vy")
    a = j // CORES
    c = j % CORES
    me = i * CORES + c
    vx_peers = [lax.rem(i + d, nx) for d in range(1, nx)]
    a_peers = [lax.rem(a + d, na) for d in range(1, na)]
    vy_peers = [lax.rem(j + d, ny) for d in range(1, ny)]
    nplane = nx * CORES
    plane = [lax.rem(me + d, nplane) for d in range(1, nplane)]

    def remote(src, dst, ss, rs, x, y):
        return pltpu.make_async_remote_copy(
            src_ref=src, dst_ref=dst, send_sem=ss, recv_sem=rs,
            device_id=(x, y), device_id_type=MESH)

    sent = []

    def send(*args):
        copy = remote(*args)
        copy.start()
        sent.append(copy)

    def arrived(ref, ss, rs):
        remote(ref, ref, ss, rs, i, j).wait_recv()

    row_j = pl.ds(pl.multiple_of(j * rows, rows), rows)
    pairs = ((wk_any, wk), (qry_any, qry), (wv_any, wbuf.at[row_j, :]), (tok_any, tok),
             (emb_any, emb), (slot_any, slot), (wo_any, wo))
    loads = [pltpu.make_async_copy(src, dst, load_s.at[n]) for n, (src, dst) in enumerate(pairs)]
    for load in loads:
        load.start()

    barrier = pltpu.get_barrier_semaphore()
    for y in vy_peers:
        pl.semaphore_signal(barrier, inc=1, device_id=(i, y), device_id_type=MESH)
    for x in vx_peers:
        for d in range(CORES):
            pl.semaphore_signal(barrier, inc=1, device_id=(x, a * CORES + d), device_id_type=MESH)

    loads[0].wait()
    loads[1].wait()
    head_row = lax.broadcasted_iota(jnp.int32, (heads, width), 0)
    head_col = lax.broadcasted_iota(jnp.int32, (heads, width), 1) // hdim
    qmat = jnp.where(head_row == head_col, jnp.broadcast_to(qry[...].astype(F32).reshape(1, width), (heads, width)), 0.0).astype(BF16)
    kq = lax.dot_general(qmat, wk[...], NT, preferred_element_type=F32)
    kq_high, kq_low = split(kq)
    kq_mine[0] = kq_high
    kq_mine[1] = kq_low

    pl.semaphore_wait(barrier, (ny - 1) + (nx - 1) * CORES)

    for y in vy_peers:
        send(kq_mine, kq_in.at[j], kq_s, kq_r.at[j], i, y)

    def block(x, d, q, n):
        first = pl.multiple_of((x * CORES + d) * rows + q * piece, piece)
        return wbuf.at[pl.ds(first, piece), pl.ds(pl.multiple_of(n * wide, wide), wide)]

    def turn(x, step):
        return lax.rem(x + 1 + step, na)

    partner = a * CORES + (1 - c)
    loads[2].wait()
    for step in range(na):
        for x in a_peers:
            n = turn(x, step)
            send(block(a, c, i, n), block(a, c, i, n), w_s, w_r.at[0, a, i, n], i, x * CORES + c)
    send(wbuf.at[row_j, :], wbuf.at[row_j, :], wp_s, wp_r, i, partner)

    kq_in[j] = kq_mine[...]

    for load in loads[3:]:
        load.wait()
    count = slot.shape[1]
    ids = (i * ny + j) * slots + lax.broadcasted_iota(jnp.int32, (8, count), 0)
    match = jnp.where(ids == jnp.broadcast_to(slot[...], (8, count)), 1.0, 0.0)
    held = jnp.max(match, axis=1, keepdims=True)
    embed = dot(match.astype(BF16), emb[...])
    for s in range(slots):
        mixed[s * patches:(s + 1) * patches, :] = (tok[s].astype(F32) + embed[s:s + 1, :]).astype(BF16)

    for y in vy_peers:
        arrived(kq_in.at[y], kq_s, kq_r.at[y])
    for y in range(ny):
        kq_all[:, :, y * rows:(y + 1) * rows] = kq_in[y]
    scores = []
    top = jnp.full((patches, heads), LOWEST, F32)
    for s in range(slots):
        rows_s = mixed[s * patches:(s + 1) * patches, :]
        score = scale * (lax.dot_general(rows_s, kq_all[0], NT, preferred_element_type=F32)
                         + lax.dot_general(rows_s, kq_all[1], NT, preferred_element_type=F32))
        score = jnp.where(held[s:s + 1, :] > 0, score, LOWEST)
        scores.append(score)
        top = jnp.maximum(top, score)
    total = jnp.zeros((patches, heads), F32)
    for s in range(slots):
        e = jnp.where(held[s:s + 1, :] > 0, jnp.exp(scores[s] - top), 0.0).astype(BF16)
        ex[s * patches:(s + 1) * patches, :] = e
        total += e.astype(F32)
    stat[:, 0:heads] = top
    stat[:, heads:2 * heads] = total

    def group_rows(x):
        return pl.ds(pl.multiple_of(x * group, group), group)

    for p in plane:
        x = p // CORES
        send(stat.at[group_rows(x), :], st_in.at[me], st_s, st_r.at[me], x, a * CORES + p % CORES)
    st_in[me] = stat[group_rows(i), :]

    def share(step):
        n = turn(a, step)
        for x in a_peers:
            here = block(x, c, i, n)
            arrived(here, w_s, w_r.at[0, x, i, n])
            for q in vx_peers:
                send(here, here, w_s, w_r.at[0, x, i, n], q, j)
            send(here, here, w_s, w_r.at[1, x, i, n], i, partner)

    def hand_over(step):
        n = turn(a, step)
        for x in a_peers:
            for q in vx_peers:
                here = block(x, c, q, n)
                arrived(here, w_s, w_r.at[0, x, q, n])
                send(here, here, w_s, w_r.at[1, x, q, n], i, partner)

    def complete(step):
        n = turn(a, step)
        for x in a_peers:
            for q in range(nx):
                arrived(block(x, 1 - c, q, n), w_s, w_r.at[1, x, q, n])

    share(0)
    if na > 1:
        share(1)
    hand_over(0)

    for p in plane:
        arrived(st_in.at[p], st_s, st_r.at[p])
    tops = [st_in[p][:, 0:heads] for p in range(nplane)]
    high = functools.reduce(jnp.maximum, tops)
    st2[:, 0:heads] = high
    st2[:, heads:2 * heads] = sum(
        jnp.exp(tops[p] - high) * st_in[p][:, heads:2 * heads] for p in range(nplane))
    for x in a_peers:
        send(st2, st2_in.at[a], st2_s, st2_r.at[a], i, x * CORES + c)
    st2_in[a] = st2[...]

    order = a_peers + [a]

    def project(x):
        start = pl.multiple_of(x * wide, wide)
        col = start + lax.broadcasted_iota(jnp.int32, (heads, wide), 1)
        to_cols = jnp.where(col // hdim == lax.broadcasted_iota(jnp.int32, (heads, wide), 0), 1.0, 0.0).astype(BF16)
        value = dot(mixed[...], wbuf[:, pl.ds(start, wide)])
        value = value * dot(ex[...], to_cols)
        context = sum(value[s * patches:(s + 1) * patches] for s in range(slots)).astype(BF16)
        for g in range(nx):
            for d in range(CORES):
                part[x, g * CORES + d] = context[g * group:(g + 1) * group, d * rows:(d + 1) * rows]
        for p in plane:
            send(part.at[x, p], in1.at[x, me], s1_s, s1_r.at[x, me], p // CORES, a * CORES + p % CORES)

    def combine(x, last):
        for p in plane:
            arrived(in1.at[x, p], s1_s, s1_r.at[x, p])
        acc = fexp[x, me] * part[x, me].astype(F32)
        for p in plane:
            acc += fexp[x, p] * in1[x, p].astype(F32)
        if last:
            return acc
        p2[x] = acc.astype(BF16)
        send(p2.at[x], in2.at[a], s2_s, s2_r.at[a], i, x * CORES + c)

    arrived(wbuf.at[pl.ds(pl.multiple_of(partner * rows, rows), rows), :], wp_s, wp_r)
    complete(0)
    project(order[0])
    if na > 2:
        share(2)
    if na > 1:
        hand_over(1)

    for x in a_peers:
        arrived(st2_in.at[x], st2_s, st2_r.at[x])
    highest = functools.reduce(jnp.maximum, [st2_in[p][:, 0:heads] for p in range(na)])
    whole = sum(jnp.exp(st2_in[p][:, 0:heads] - highest) * st2_in[p][:, heads:2 * heads] for p in range(na))
    k = lax.broadcasted_iota(jnp.int32, (heads, na * rows), 1)
    feature = ((k // rows) * CORES + c) * rows + k % rows
    spread = jnp.where(feature // hdim == lax.broadcasted_iota(jnp.int32, (heads, na * rows), 0), 1.0, 0.0).astype(BF16)
    for p in range(nplane):
        factor = jnp.exp(st_in[p][:, 0:heads] - highest) / whole
        f_high, f_low = split(factor)
        grown = dot(f_high, spread) + dot(f_low, spread)
        for x in range(na):
            fexp[x, p] = grown[:, x * rows:(x + 1) * rows]

    for n in range(1, na):
        complete(n)
        project(order[n])
        if n + 2 < na:
            share(n + 2)
        if n + 1 < na:
            hand_over(n + 1)
        combine(order[n - 1], False)
    acc = combine(a, True)
    for x in a_peers:
        arrived(in2.at[x], s2_s, s2_r.at[x])
        acc += in2[x].astype(F32)
    result = dot(acc.astype(BF16), wo[...]).astype(BF16)
    for y in range(ny):
        o3[y] = result[y * own:(y + 1) * own]
    for y in vy_peers:
        send(o3.at[y], in3.at[j], s3_s, s3_r.at[j], i, y)
    final = o3[j].astype(F32)
    for y in vy_peers:
        arrived(in3.at[y], s3_s, s3_r.at[y])
        final += in3[y].astype(F32)
    out[...] = final.astype(BF16)
    for copy in sent:
        copy.wait_send()


def shards(tokens, var_embed, query, key_weight, value_weight, out_weight, var_slot):
    slots, batch, patches, width = tokens.shape
    nx, ny = lax.axis_size("vx"), lax.axis_size("vy")
    heads = HEADS
    rows, na, group, own = width // ny, ny // CORES, patches // nx, patches // (nx * ny)
    nplane = nx * CORES
    dma = pltpu.SemaphoreType.DMA
    vmem = pltpu.VMEM
    result = pl.pallas_call(
        functools.partial(kernel, nx, ny, heads),
        out_shape=jax.ShapeDtypeStruct((own, width), BF16),
        in_specs=[pl.BlockSpec(memory_space=pl.ANY)] * 7,
        out_specs=pl.BlockSpec(memory_space=pltpu.VMEM),
        scratch_shapes=[
            vmem((slots, batch * patches, width), BF16),
            vmem(var_embed.shape, BF16),
            vmem((width,), BF16),
            vmem((rows, width), BF16),
            vmem((rows, width), BF16),
            vmem((1, var_slot.shape[0]), jnp.int32),
            dma((7,)),
            vmem((slots * patches, width), BF16),
            vmem((width, width), BF16),
            vmem((2, heads, rows), BF16),
            vmem((ny, 2, heads, rows), BF16),
            vmem((2, heads, width), BF16),
            vmem((slots * patches, heads), BF16),
            vmem((patches, 2 * heads), F32),
            vmem((nplane, group, 2 * heads), F32),
            vmem((group, 2 * heads), F32),
            vmem((na, group, 2 * heads), F32),
            vmem((na, nplane, group, rows), F32),
            vmem((na, nplane, group, rows), BF16),
            vmem((na, nplane, group, rows), BF16),
            vmem((na, group, rows), BF16),
            vmem((na, group, rows), BF16),
            vmem((ny, own, width), BF16),
            vmem((ny, own, width), BF16),
            dma, dma((ny,)),
            dma, dma((2, na, nx, na)),
            dma, dma,
            dma, dma((nplane,)),
            dma, dma((na,)),
            dma, dma((na, nplane)),
            dma, dma((na,)),
            dma, dma((ny,)),
        ],
        compiler_params=pltpu.CompilerParams(
            collective_id=0, has_side_effects=True, vmem_limit_bytes=60 * 1024 * 1024),
    )(
        tokens.reshape(slots, batch * patches, width), var_embed, query,
        key_weight, value_weight, out_weight, var_slot.reshape(1, -1),
    )
    return result.reshape(batch, -1, width)


def solution(mesh):
    placed = (
        P(("vx", "vy"), None, None, None),
        P(),
        P(),
        P("vy", None),
        P("vy", None),
        P("vy", None),
        P(),
    )
    return jax.shard_map(
        shards, mesh=mesh, in_specs=placed, out_specs=P(None, ("vx", "vy"), None), check_vma=False
    )
```

profile of v0, /device:TPU:0, one launch (start us, length us, event | category | flops | bytes accessed | tf_op | source)
XLA Modules:
  0.0 44.1 jit_solution(2454148676028063617)
XLA Ops:
  0.0 42.7 %shard_map.73 = bf16[8,1024]{1,0:T(8,128)(2,1)} custom-call(bf16[3,256,1024]{2,1,0:T(8,128)(2,1)} %bitcast.3, bf16[91,1024]{1,0:T(8,128)(2,1)} %emb_any.1, bf16[1024]{0:T(1024)(128)(2,1)} %qry_any.1, bf16[128,1024]{1,0:T(8,128)(2,1)} %wk_any.1, bf16[128,1024]{1,0:T(8,128)(2,1)} %wv_any.1, bf16[128,1024]{1,0:T(8,128)(2,1)} %wo_any.1, s32[1,91]{1,0:T(1,128)} %bitcast.5), custom_call_target="tpu_custom_call" | custom-call | tf_op jit(solution)/shard_map/pallas_call | solution.py:275
  42.7 1.3 %copy.9 = bf16[1,8,1024]{2,1,0:T(8,128)(2,1)} copy(bf16[1,8,1024]{2,1,0:T(8,128)(2,1)} %bitcast.4) | data formatting | bytes 32768
where the time goes:
time: 44.3 us; the launch traced here: 44.1 us
  Pallas kernels  42.7 us (96%)
  local copies, waits for them, and re-layouts  1.32 us (3%)
    pallas_call x1, Pallas kernels, shards(): pl.pallas_call(functools.partial(kernel, nx, ny, heads), out_shape=jax.Sh...  42.7 us
    unnamed x1, local copies, waits for them, and re-layouts  1.32 us

commit v1 on v0

v1 whole, which is shorter than its diff:
```python
import functools
import math

import jax
import jax.numpy as jnp
from jax import lax
from jax.experimental import pallas as pl
from jax.experimental.pallas import tpu as pltpu
from jax.sharding import PartitionSpec as P

HEADS = 16
CORES = 2
CHUNK = 256
LOWEST = -1e38
F32 = jnp.float32
BF16 = jnp.bfloat16
MESH = pl.DeviceIdType.MESH
NT = (((1,), (1,)), ((), ()))


def split(x):
    high = x.astype(BF16)
    return high, (x - high.astype(F32)).astype(BF16)


def dot(a, b):
    return jnp.dot(a, b, preferred_element_type=F32)


def kernel(nx, ny, heads, tok_any, emb_any, qry_any, wk_any, wv_any, wo_any, slot_any, out,
           tok, emb, qry, wk, wo, slot, mixed, wbuf, wother, kq_mine, kq_in, kq_all, ex,
           stat, st_in, st2, st2_in, fexp, part, in1, p2, in2, o3, in3,
           load_s, send_s, kq_r, z_r, w_r, tok_r, st_r, st2_r, s1_r, s2_r, s3_r):
    _, slots, patches, width = tok.shape
    rows = width // ny
    na = ny // CORES
    group = patches // nx
    piece = rows // nx
    lane = width // CORES
    chunk = min(CHUNK, lane)
    chunks = lane // chunk
    per_chunk = chunk // rows
    own = patches // (nx * ny)
    hdim = width // heads
    lheads = heads // CORES
    held_slots = CORES * slots
    block_rows = held_slots * group
    scale = 1.0 / math.sqrt(hdim)
    i = lax.axis_index("vx")
    j = lax.axis_index("vy")
    a = j // CORES
    c = j % CORES
    partner = a * CORES + (1 - c)
    x_peers = [lax.rem(i + d, nx) for d in range(1, nx)]
    a_peers = [lax.rem(a + d, na) for d in range(1, na)]
    vy_peers = [lax.rem(j + d, ny) for d in range(1, ny)]

    def remote(src, dst, rs, x, y):
        return pltpu.make_async_remote_copy(
            src_ref=src, dst_ref=dst, send_sem=send_s, recv_sem=rs,
            device_id=(x, y), device_id_type=MESH)

    sent = []

    def send(*args):
        copy = remote(*args)
        copy.start()
        sent.append(copy)

    def arrived(ref, rs):
        remote(ref, ref, rs, i, j).wait_recv()

    def half(which):
        return wv_any.at[:, pl.ds(pl.multiple_of(which * lane, lane), lane)]

    pairs = ((wk_any, wk), (qry_any, qry), (half(c), wbuf.at[j]), (half(1 - c), wother),
             (tok_any, tok.at[c]), (emb_any, emb), (slot_any, slot), (wo_any, wo))
    loads = [pltpu.make_async_copy(src, dst, load_s.at[n]) for n, (src, dst) in enumerate(pairs)]
    for load in loads:
        load.start()

    barrier = pltpu.get_barrier_semaphore()
    for y in vy_peers:
        pl.semaphore_signal(barrier, inc=1, device_id=(i, y), device_id_type=MESH)
    for x in x_peers:
        pl.semaphore_signal(barrier, inc=1, device_id=(x, j), device_id_type=MESH)

    with jax.named_scope("A_load01"):
        loads[0].wait()
        loads[1].wait()
    head_row = lax.broadcasted_iota(jnp.int32, (heads, width), 0)
    head_col = lax.broadcasted_iota(jnp.int32, (heads, width), 1) // hdim
    qmat = jnp.where(head_row == head_col, jnp.broadcast_to(qry[...].astype(F32).reshape(1, width), (heads, width)), 0.0).astype(BF16)
    kq = lax.dot_general(qmat, wk[...], NT, preferred_element_type=F32)
    for d in range(CORES):
        kq_high, kq_low = split(kq[d * lheads:(d + 1) * lheads])
        kq_mine[d, 0] = kq_high
        kq_mine[d, 1] = kq_low

    with jax.named_scope("B_barrier"):
        pl.semaphore_wait(barrier, (ny - 1) + (nx - 1))

    for y in vy_peers:
        send(kq_mine.at[y % CORES], kq_in.at[j], kq_r, i, y)

    def cols(n):
        return pl.ds(n * chunk, chunk)

    def piece_rows(q):
        return pl.ds(pl.multiple_of(q * piece, piece), piece)

    with jax.named_scope("C_load23"):
        loads[2].wait()
        loads[3].wait()
    for n in range(chunks):
        for x in a_peers:
            here = wbuf.at[j, piece_rows(i), cols(n)]
            send(here, here, z_r.at[n, a], i, x * CORES + c)
            send(wother.at[piece_rows(i), cols(n)], here, z_r.at[n, a], i, x * CORES + (1 - c))
        send(wother.at[:, cols(n)], wbuf.at[j, :, cols(n)], w_r.at[n, a], i, partner)
    with jax.named_scope("C_load4"):
        loads[4].wait()
    send(tok.at[c], tok.at[c], tok_r, i, partner)

    kq_in[j] = kq_mine[c]

    def pair_rows(x, q, n):
        return wbuf.at[pl.ds(pl.multiple_of(x * CORES, CORES), CORES), piece_rows(q), cols(n)]

    def share(n):
        for x in a_peers:
            here = pair_rows(x, i, n)
            arrived(here, z_r.at[n, x])
            for q in x_peers:
                send(here, here, w_r.at[n, x], q, j)

    def complete(n):
        arrived(wbuf.at[partner, :, cols(n)], w_r.at[n, a])
        for x in a_peers:
            arrived(wbuf.at[pl.ds(pl.multiple_of(x * CORES, CORES), CORES), 0:(nx - 1) * piece, cols(n)], w_r.at[n, x])

    with jax.named_scope("D_loads"):
        for load in loads[5:]:
            load.wait()
    count = slot.shape[1]
    padded = -(-held_slots // 8) * 8
    ids = (i * ny + a * CORES) * slots + lax.broadcasted_iota(jnp.int32, (padded, count), 0)
    match = jnp.where(ids == jnp.broadcast_to(slot[...], (padded, count)), 1.0, 0.0)
    held = jnp.max(match, axis=1, keepdims=True)
    embed = dot(match.astype(BF16), emb[...])

    def mix(core):
        for s in range(slots):
            m = core * slots + s
            line = jnp.sum(jnp.where(lax.broadcasted_iota(jnp.int32, (padded, width), 0) == m, embed, 0.0), axis=0, keepdims=True)
            for g in range(nx):
                first = pl.multiple_of(g * block_rows + m * group, group)
                mixed[pl.ds(first, group), :] = (tok[core, s, g * group:(g + 1) * group, :].astype(F32) + line).astype(BF16)

    with jax.named_scope("E_mix"):
        mix(c)
    with jax.named_scope("F_share0"):
        share(0)
    with jax.named_scope("G_tok"):
        arrived(tok.at[1 - c], tok_r)
    with jax.named_scope("G_mix2"):
        mix(1 - c)

    with jax.named_scope("H_kq"):
        arrived(kq_in.at[0:ny - 1], kq_r)
    for y in range(ny):
        for d in range(2):
            kq_all[d * lheads:(d + 1) * lheads, y * rows:(y + 1) * rows] = kq_in[y, d]
    for g in range(nx):
        both = lax.dot_general(mixed[g * block_rows:(g + 1) * block_rows, :], kq_all[...], NT, preferred_element_type=F32)
        score = scale * (both[:, 0:lheads] + both[:, lheads:2 * lheads])
        top = jnp.full((group, lheads), LOWEST, F32)
        scores = []
        for s in range(held_slots):
            here = jnp.where(held[s:s + 1, :] > 0, score[s * group:(s + 1) * group], LOWEST)
            scores.append(here)
            top = jnp.maximum(top, here)
        total = jnp.zeros((group, lheads), F32)
        for s in range(held_slots):
            e = jnp.where(held[s:s + 1, :] > 0, jnp.exp(scores[s] - top), 0.0).astype(BF16)
            ex[g * block_rows + s * group:g * block_rows + (s + 1) * group, :] = e
            total += e.astype(F32)
        stat[g, :, 0:lheads] = top
        stat[g, :, lheads:2 * lheads] = total

    for q in x_peers:
        send(stat.at[q], st_in.at[i], st_r, q, j)
    st_in[i] = stat[i]

    with jax.named_scope("J_share1"):
        for n in range(1, chunks):
            share(n)

    with jax.named_scope("K_st"):
        arrived(st_in.at[0:nx - 1], st_r)
    tops = [st_in[q][:, 0:lheads] for q in range(nx)]
    high = functools.reduce(jnp.maximum, tops)
    st2[:, 0:lheads] = high
    st2[:, lheads:2 * lheads] = sum(
        jnp.exp(tops[q] - high) * st_in[q][:, lheads:2 * lheads] for q in range(nx))
    for x in a_peers:
        send(st2, st2_in.at[a], st2_r, i, x * CORES + c)
    st2_in[a] = st2[...]

    def project(n):
        col = n * chunk + lax.broadcasted_iota(jnp.int32, (lheads, chunk), 1)
        to_cols = jnp.where(col // hdim == lax.broadcasted_iota(jnp.int32, (lheads, chunk), 0), 1.0, 0.0).astype(BF16)
        for g in x_peers + [i]:
            here = pl.ds(pl.multiple_of(g * block_rows, block_rows), block_rows)
            value = dot(mixed[here, :], wbuf[:, :, n * chunk:(n + 1) * chunk].reshape(width, chunk))
            value = value * dot(ex[here, :], to_cols)
            context = sum(value[s * group:(s + 1) * group] for s in range(held_slots)).astype(BF16)
            if g is i:
                in1[n, i] = context
            else:
                part[n, g] = context
                send(part.at[n, g], in1.at[n, i], s1_r.at[n], g, j)

    def combine(n):
        arrived(in1.at[n, 0:nx - 1], s1_r.at[n])
        acc = sum(fexp[q, :, n * chunk:(n + 1) * chunk] * in1[n, q].astype(F32) for q in range(nx))
        for k in range(per_chunk):
            b = n * per_chunk + k
            p2[b] = acc[:, k * rows:(k + 1) * rows].astype(BF16)
            target = c * na + b

            @pl.when(target != j)
            def _():
                remote(p2.at[b], in2.at[a], s2_r, i, target).start()

    with jax.named_scope("L_complete0"):
        complete(0)
    with jax.named_scope("M_project0"):
        project(0)

    with jax.named_scope("N_st2"):
        arrived(st2_in.at[0:na - 1], st2_r)
    highest = functools.reduce(jnp.maximum, [st2_in[p][:, 0:lheads] for p in range(na)])
    whole = sum(jnp.exp(st2_in[p][:, 0:lheads] - highest) * st2_in[p][:, lheads:2 * lheads] for p in range(na))
    feature = lax.broadcasted_iota(jnp.int32, (lheads, lane), 1)
    spread = jnp.where(feature // hdim == lax.broadcasted_iota(jnp.int32, (lheads, lane), 0), 1.0, 0.0).astype(BF16)
    for q in range(nx):
        f_high, f_low = split(jnp.exp(st_in[q][:, 0:lheads] - highest) / whole)
        fexp[q] = dot(f_high, spread) + dot(f_low, spread)

    for n in range(1, chunks):
        with jax.named_scope("O_complete"):
            complete(n)
        with jax.named_scope("P_project"):
            project(n)
        with jax.named_scope("Q_combine0"):
            combine(n - 1)
    with jax.named_scope("R_combine1"):
        combine(chunks - 1)

    mine = j // na == c

    @pl.when(mine)
    def _():
        in2[a] = p2[lax.rem(j, na)]
        arrived(in2.at[0:na - 1], s2_r)

    @pl.when(jnp.logical_not(mine))
    def _():
        arrived(in2, s2_r)

    acc = sum(in2[x].astype(F32) for x in range(na))
    result = dot(acc.astype(BF16), wo[...]).astype(BF16)
    for y in range(ny):
        o3[y] = result[y * own:(y + 1) * own]
    for y in vy_peers:
        send(o3.at[y], in3.at[j], s3_r, i, y)
    final = o3[j].astype(F32)
    with jax.named_scope("T_in3"):
        arrived(in3.at[0:ny - 1], s3_r)
    for y in vy_peers:
        final += in3[y].astype(F32)
    out[...] = final.astype(BF16)
    with jax.named_scope("U_sends"):
        for copy in sent:
            copy.wait_send()
    for b in range(chunks * per_chunk):
        @pl.when(c * na + b != j)
        def _():
            remote(p2.at[b], in2.at[a], s2_r, i, c * na + b).wait_send()


def shards(tokens, var_embed, query, key_weight, value_weight, out_weight, var_slot):
    slots, batch, patches, width = tokens.shape
    nx, ny = lax.axis_size("vx"), lax.axis_size("vy")
    heads = HEADS
    patches = batch * patches
    rows, na, group, own = width // ny, ny // CORES, patches // nx, patches // (nx * ny)
    lane, lheads = width // CORES, heads // CORES
    chunk = min(CHUNK, lane)
    chunks = lane // chunk
    held = CORES * slots * patches
    dma = pltpu.SemaphoreType.DMA
    vmem = pltpu.VMEM
    result = pl.pallas_call(
        functools.partial(kernel, nx, ny, heads),
        out_shape=vmem((own, width), BF16),
        in_specs=[pl.BlockSpec(memory_space=pl.ANY)] * 7,
        out_specs=pl.BlockSpec(memory_space=vmem),
        scratch_shapes=[
            vmem((CORES, slots, patches, width), BF16),
            vmem(var_embed.shape, BF16),
            vmem((width,), BF16),
            vmem((rows, width), BF16),
            vmem((rows, width), BF16),
            vmem((1, var_slot.shape[0]), jnp.int32),
            vmem((held, width), BF16),
            vmem((ny, rows, lane), BF16),
            vmem((rows, lane), BF16),
            vmem((CORES, 2, lheads, rows), BF16),
            vmem((ny, 2, lheads, rows), BF16),
            vmem((2 * lheads, width), BF16),
            vmem((held, lheads), BF16),
            vmem((nx, group, 2 * lheads), F32),
            vmem((nx, group, 2 * lheads), F32),
            vmem((group, 2 * lheads), F32),
            vmem((na, group, 2 * lheads), F32),
            vmem((nx, group, lane), F32),
            vmem((chunks, nx, group, chunk), BF16),
            vmem((chunks, nx, group, chunk), BF16),
            vmem((na, group, rows), BF16),
            vmem((na, group, rows), BF16),
            vmem((ny, own, width), BF16),
            vmem((ny, own, width), BF16),
            dma((8,)), dma, dma, dma((chunks, na)), dma((chunks, na)), dma, dma, dma,
            dma((chunks,)), dma, dma,
        ],
        compiler_params=pltpu.CompilerParams(
            collective_id=0, has_side_effects=True, vmem_limit_bytes=56 * 1024 * 1024),
    )(
        tokens.reshape(slots, patches, width), var_embed, query,
        key_weight, value_weight, out_weight, var_slot.reshape(1, -1),
    )
    return result.reshape(batch, -1, width)


def solution(mesh):
    placed = (
        P(("vx", "vy"), None, None, None),
        P(),
        P(),
        P("vy", None),
        P("vy", None),
        P("vy", None),
        P(),
    )
    return jax.shard_map(
        shards, mesh=mesh, in_specs=placed, out_specs=P(None, ("vx", "vy"), None), check_vma=False
    )
```

time: 44.3 us -> 36.6 us (0.83)
  Pallas kernels: 42.7 us -> 35.9 us
  local copies, waits for them, and re-layouts: 1.32 us -> 0.61 us
    pallas_call x1, Pallas kernels: 42.7 us -> 35.9 us  [shards(): pl.pallas_call(functools.partial(kernel, nx, ny, heads), out_shape=vmem((...]
    unnamed x1, local copies, waits for them, and re-layouts: 1.32 us -> 0.61 us
where the time goes in v1:
time: 36.6 us; the launch traced here: 36.5 us
  Pallas kernels  35.9 us (98%)
  local copies, waits for them, and re-layouts  0.61 us (2%)
    pallas_call x1, Pallas kernels, shards(): pl.pallas_call(functools.partial(kernel, nx, ny, heads), out_shape=vmem((...  35.9 us

profile of v1, /device:TPU:0, one launch (start us, length us, event | category | flops | bytes accessed | tf_op | source)
XLA Modules:
  0.0 36.5 jit_solution(4840424788830011012)
XLA Ops:
  0.0 35.9 %shard_map.73 = bf16[8,1024]{1,0:T(8,128)(2,1)S(1)} custom-call(bf16[3,256,1024]{2,1,0:T(8,128)(2,1)} %bitcast.4, bf16[91,1024]{1,0:T(8,128)(2,1)} %emb_any.1, bf16[1024]{0:T(1024)(128)(2,1)} %qry_any.1, bf16[128,1024]{1,0:T(8,128)(2,1)} %wk_any.1, bf16[128,1024]{1,0:T(8,128)(2,1)} %wv_any.1, bf16[128,1024]{1,0:T(8,128)(2,1)} %wo_any.1, s32[1,91]{1,0:T(1,128)} %bitcast.5), custom_call_target="tpu_custom_call" | custom-call | tf_op jit(solution)/shard_map/pallas_call | solution.py:305
  35.9 0.6 %copy.9 = bf16[1,8,1024]{2,1,0:T(8,128)(2,1)} copy(bf16[1,8,1024]{2,1,0:T(8,128)(2,1)S(1)} %bitcast.3) | data formatting | bytes 32768

commit v2 on v1

--- a/solution.py
+++ b/solution.py
@@ -27,10 +27,19 @@
     return jnp.dot(a, b, preferred_element_type=F32)
 
 
+def flip(index, mask, size):
+    bit = 1
+    while bit < size:
+        if mask & bit:
+            index = index + bit - 2 * bit * (index // bit % 2)
+        bit *= 2
+    return index
+
+
 def kernel(nx, ny, heads, tok_any, emb_any, qry_any, wk_any, wv_any, wo_any, slot_any, out,
            tok, emb, qry, wk, wo, slot, mixed, wbuf, wother, kq_mine, kq_in, kq_all, ex,
            stat, st_in, st2, st2_in, fexp, part, in1, p2, in2, o3, in3,
-           load_s, send_s, kq_r, z_r, w_r, tok_r, st_r, st2_r, s1_r, s2_r, s3_r):
+           load_s, send_s, kq_r, z_r, w_r, tok_r, wo_r, st_r, st2_r, s1_r, s2_r, s3_r):
     _, slots, patches, width = tok.shape
     rows = width // ny
     na = ny // CORES
@@ -39,7 +48,9 @@
     lane = width // CORES
     chunk = min(CHUNK, lane)
     chunks = lane // chunk
-    per_chunk = chunk // rows
+    wide = CORES * rows
+    per_chunk = chunk // wide
+    first_plane = na // CORES
     own = patches // (nx * ny)
     hdim = width // heads
     lheads = heads // CORES
@@ -51,8 +62,9 @@
     a = j // CORES
     c = j % CORES
     partner = a * CORES + (1 - c)
-    x_peers = [lax.rem(i + d, nx) for d in range(1, nx)]
-    a_peers = [lax.rem(a + d, na) for d in range(1, na)]
+    x_peers = [flip(i, d, nx) for d in range(1, nx)]
+    mirror = x_peers[-1]
+    a_peers = [flip(a, d, na) for d in range(1, na)]
     vy_peers = [lax.rem(j + d, ny) for d in range(1, ny)]
 
     def remote(src, dst, rs, x, y):
@@ -74,7 +86,7 @@
         return wv_any.at[:, pl.ds(pl.multiple_of(which * lane, lane), lane)]
 
     pairs = ((wk_any, wk), (qry_any, qry), (half(c), wbuf.at[j]), (half(1 - c), wother),
-             (tok_any, tok.at[c]), (emb_any, emb), (slot_any, slot), (wo_any, wo))
+             (tok_any, tok.at[c]), (emb_any, emb), (slot_any, slot), (wo_any, wo.at[c]))
     loads = [pltpu.make_async_copy(src, dst, load_s.at[n]) for n, (src, dst) in enumerate(pairs)]
     for load in loads:
         load.start()
@@ -112,12 +124,17 @@
     with jax.named_scope("C_load23"):
         loads[2].wait()
         loads[3].wait()
+    def along_z(q, n, sem):
+        for x in a_peers:
+            here = wbuf.at[j, piece_rows(q), cols(n)]
+            send(here, here, sem, i, x * CORES + c)
+            send(wother.at[piece_rows(q), cols(n)], here, sem, i, x * CORES + (1 - c))
+
     for n in range(chunks):
-        for x in a_peers:
-            here = wbuf.at[j, piece_rows(i), cols(n)]
-            send(here, here, z_r.at[n, a], i, x * CORES + c)
-            send(wother.at[piece_rows(i), cols(n)], here, z_r.at[n, a], i, x * CORES + (1 - c))
+        along_z(i, n, z_r.at[n, a])
         send(wother.at[:, cols(n)], wbuf.at[j, :, cols(n)], w_r.at[n, a], i, partner)
+    for n in range(1, chunks):
+        along_z(mirror, n, w_r.at[n, a])
     with jax.named_scope("C_load4"):
         loads[4].wait()
     send(tok.at[c], tok.at[c], tok_r, i, partner)
@@ -127,12 +144,11 @@
     def pair_rows(x, q, n):
         return wbuf.at[pl.ds(pl.multiple_of(x * CORES, CORES), CORES), piece_rows(q), cols(n)]
 
-    def share(n):
-        for x in a_peers:
-            here = pair_rows(x, i, n)
-            arrived(here, z_r.at[n, x])
-            for q in x_peers:
-                send(here, here, w_r.at[n, x], q, j)
+    def share(n, x):
+        here = pair_rows(x, i, n)
+        arrived(here, z_r.at[n, x])
+        for q in x_peers if n == 0 else x_peers[:-1]:
+            send(here, here, w_r.at[n, x], q, j)
 
     def complete(n):
         arrived(wbuf.at[partner, :, cols(n)], w_r.at[n, a])
@@ -157,15 +173,18 @@
                 first = pl.multiple_of(g * block_rows + m * group, group)
                 mixed[pl.ds(first, group), :] = (tok[core, s, g * group:(g + 1) * group, :].astype(F32) + line).astype(BF16)
 
+    send(wo.at[c], wo.at[c], wo_r, i, partner)
     with jax.named_scope("E_mix"):
         mix(c)
-    with jax.named_scope("F_share0"):
-        share(0)
+    with jax.named_scope("F_share00"):
+        share(0, a_peers[0])
     with jax.named_scope("G_tok"):
         arrived(tok.at[1 - c], tok_r)
     with jax.named_scope("G_mix2"):
         mix(1 - c)
-
+    with jax.named_scope("G_share01"):
+        for x in a_peers[1:-1]:
+            share(0, x)
     with jax.named_scope("H_kq"):
         arrived(kq_in.at[0:ny - 1], kq_r)
     for y in range(ny):
@@ -192,9 +211,41 @@
         send(stat.at[q], st_in.at[i], st_r, q, j)
     st_in[i] = stat[i]
 
+    with jax.named_scope("J_share02"):
+        share(0, a_peers[-1])
     with jax.named_scope("J_share1"):
         for n in range(1, chunks):
-            share(n)
+            for x in a_peers:
+                share(n, x)
+
+    def project(n):
+        col = n * chunk + lax.broadcasted_iota(jnp.int32, (lheads, chunk), 1)
+        to_cols = jnp.where(col // hdim == lax.broadcasted_iota(jnp.int32, (lheads, chunk), 0), 1.0, 0.0).astype(BF16)
+        weight = wbuf[:, :, n * chunk:(n + 1) * chunk].reshape(width, chunk)
+        for g in range(nx):
+            here = slice(g * block_rows, (g + 1) * block_rows)
+            value = dot(mixed[here, :], weight) * dot(ex[here, :], to_cols)
+            part[n, g] = sum(value[s * group:(s + 1) * group] for s in range(held_slots)).astype(BF16)
+        for q in x_peers:
+            send(part.at[n, q], in1.at[n, i], s1_r.at[n], q, j)
+
+    def combine(n):
+        arrived(in1.at[n, 0:nx - 1], s1_r.at[n])
+        here = slice(n * chunk, (n + 1) * chunk)
+        acc = fexp[i, :, here] * part[n, i].astype(F32)
+        for q in x_peers:
+            acc += fexp[q, :, here] * in1[n, q].astype(F32)
+        for k in range(per_chunk):
+            b = n * per_chunk + k
+            block = acc[:, k * wide:(k + 1) * wide]
+            for d in range(CORES):
+                picked = [block[(x * CORES + d) * own:(x * CORES + d + 1) * own] for x in range(na)]
+                p2[b, d] = jnp.concatenate(picked, axis=0).astype(BF16)
+                target = (c * first_plane + b) * CORES + d
+
+                @pl.when(target != j)
+                def _():
+                    remote(p2.at[b, d], in2.at[a], s2_r, i, target).start()
 
     with jax.named_scope("K_st"):
         arrived(st_in.at[0:nx - 1], st_r)
@@ -207,37 +258,16 @@
         send(st2, st2_in.at[a], st2_r, i, x * CORES + c)
     st2_in[a] = st2[...]
 
-    def project(n):
-        col = n * chunk + lax.broadcasted_iota(jnp.int32, (lheads, chunk), 1)
-        to_cols = jnp.where(col // hdim == lax.broadcasted_iota(jnp.int32, (lheads, chunk), 0), 1.0, 0.0).astype(BF16)
-        for g in x_peers + [i]:
-            here = pl.ds(pl.multiple_of(g * block_rows, block_rows), block_rows)
-            value = dot(mixed[here, :], wbuf[:, :, n * chunk:(n + 1) * chunk].reshape(width, chunk))
-            value = value * dot(ex[here, :], to_cols)
-            context = sum(value[s * group:(s + 1) * group] for s in range(held_slots)).astype(BF16)
-            if g is i:
-                in1[n, i] = context
-            else:
-                part[n, g] = context
-                send(part.at[n, g], in1.at[n, i], s1_r.at[n], g, j)
-
-    def combine(n):
-        arrived(in1.at[n, 0:nx - 1], s1_r.at[n])
-        acc = sum(fexp[q, :, n * chunk:(n + 1) * chunk] * in1[n, q].astype(F32) for q in range(nx))
-        for k in range(per_chunk):
-            b = n * per_chunk + k
-            p2[b] = acc[:, k * rows:(k + 1) * rows].astype(BF16)
-            target = c * na + b
-
-            @pl.when(target != j)
-            def _():
-                remote(p2.at[b], in2.at[a], s2_r, i, target).start()
-
     with jax.named_scope("L_complete0"):
         complete(0)
     with jax.named_scope("M_project0"):
         project(0)
 
+    for n in range(1, chunks):
+        with jax.named_scope("O_complete"):
+            complete(n)
+        with jax.named_scope("P_project"):
+            project(n)
     with jax.named_scope("N_st2"):
         arrived(st2_in.at[0:na - 1], st2_r)
     highest = functools.reduce(jnp.maximum, [st2_in[p][:, 0:lheads] for p in range(na)])
@@ -248,21 +278,15 @@
         f_high, f_low = split(jnp.exp(st_in[q][:, 0:lheads] - highest) / whole)
         fexp[q] = dot(f_high, spread) + dot(f_low, spread)
 
-    for n in range(1, chunks):
-        with jax.named_scope("O_complete"):
-            complete(n)
-        with jax.named_scope("P_project"):
-            project(n)
-        with jax.named_scope("Q_combine0"):
-            combine(n - 1)
-    with jax.named_scope("R_combine1"):
-        combine(chunks - 1)
-
-    mine = j // na == c
+    for n in range(chunks):
+        with jax.named_scope(f"R_combine{n}"):
+            combine(n)
+
+    mine = a // first_plane == c
 
     @pl.when(mine)
     def _():
-        in2[a] = p2[lax.rem(j, na)]
+        in2[a] = p2[lax.rem(a, first_plane), c]
         arrived(in2.at[0:na - 1], s2_r)
 
     @pl.when(jnp.logical_not(mine))
@@ -270,24 +294,28 @@
         arrived(in2, s2_r)
 
     acc = sum(in2[x].astype(F32) for x in range(na))
-    result = dot(acc.astype(BF16), wo[...]).astype(BF16)
-    for y in range(ny):
-        o3[y] = result[y * own:(y + 1) * own]
-    for y in vy_peers:
-        send(o3.at[y], in3.at[j], s3_r, i, y)
-    final = o3[j].astype(F32)
+    arrived(wo.at[1 - c], wo_r)
+    result = dot(acc.astype(BF16), wo[...].reshape(wide, width)).astype(BF16)
+    for x in range(na):
+        o3[x] = result[x * own:(x + 1) * own]
+    for x in a_peers:
+        send(o3.at[x], in3.at[a], s3_r, i, x * CORES + c)
+    final = o3[a].astype(F32)
     with jax.named_scope("T_in3"):
-        arrived(in3.at[0:ny - 1], s3_r)
-    for y in vy_peers:
-        final += in3[y].astype(F32)
+        arrived(in3.at[0:na - 1], s3_r)
+    for x in a_peers:
+        final += in3[x].astype(F32)
     out[...] = final.astype(BF16)
     with jax.named_scope("U_sends"):
         for copy in sent:
             copy.wait_send()
     for b in range(chunks * per_chunk):
-        @pl.when(c * na + b != j)
-        def _():
-            remote(p2.at[b], in2.at[a], s2_r, i, c * na + b).wait_send()
+        for d in range(CORES):
+            target = (c * first_plane + b) * CORES + d
+
+            @pl.when(target != j)
+            def _():
+                remote(p2.at[b, d], in2.at[a], s2_r, i, target).wait_send()
 
 
 def shards(tokens, var_embed, query, key_weight, value_weight, out_weight, var_slot):
@@ -312,7 +340,7 @@
             vmem(var_embed.shape, BF16),
             vmem((width,), BF16),
             vmem((rows, width), BF16),
-            vmem((rows, width), BF16),
+            vmem((CORES, rows, width), BF16),
             vmem((1, var_slot.shape[0]), jnp.int32),
             vmem((held, width), BF16),
             vmem((ny, rows, lane), BF16),
@@ -328,11 +356,11 @@
             vmem((nx, group, lane), F32),
             vmem((chunks, nx, group, chunk), BF16),
             vmem((chunks, nx, group, chunk), BF16),
-            vmem((na, group, rows), BF16),
-            vmem((na, group, rows), BF16),
-            vmem((ny, own, width), BF16),
-            vmem((ny, own, width), BF16),
-            dma((8,)), dma, dma, dma((chunks, na)), dma((chunks, na)), dma, dma, dma,
+            vmem((na // CORES, CORES, na * own, CORES * rows), BF16),
+            vmem((na, na * own, CORES * rows), BF16),
+            vmem((na, own, width), BF16),
+            vmem((na, own, width), BF16),
+            dma((8,)), dma, dma, dma((chunks, na)), dma((chunks, na)), dma, dma, dma, dma,
             dma((chunks,)), dma, dma,
         ],
         compiler_params=pltpu.CompilerParams(

time: 36.6 us -> 31.6 us (0.86)
  Pallas kernels: 35.9 us -> 30.8 us
    pallas_call x1, Pallas kernels: 35.9 us -> 30.8 us  [shards(): pl.pallas_call(functools.partial(kernel, nx, ny, heads), out_shape=vmem((...]
where the time goes in v2:
time: 31.6 us; the launch traced here: 31.4 us
  Pallas kernels  30.8 us (97%)
  local copies, waits for them, and re-layouts  0.61 us (2%)
    pallas_call x1, Pallas kernels, shards(): pl.pallas_call(functools.partial(kernel, nx, ny, heads), out_shape=vmem((...  30.8 us

profile of v2, /device:TPU:0, one launch (start us, length us, event | category | flops | bytes accessed | tf_op | source)
XLA Modules:
  0.0 31.4 jit_solution(8184438394488891923)
XLA Ops:
  0.0 30.8 %shard_map.73 = bf16[8,1024]{1,0:T(8,128)(2,1)S(1)} custom-call(bf16[3,256,1024]{2,1,0:T(8,128)(2,1)} %bitcast.4, bf16[91,1024]{1,0:T(8,128)(2,1)} %emb_any.1, bf16[1024]{0:T(1024)(128)(2,1)} %qry_any.1, bf16[128,1024]{1,0:T(8,128)(2,1)} %wk_any.1, bf16[128,1024]{1,0:T(8,128)(2,1)} %wv_any.1, bf16[128,1024]{1,0:T(8,128)(2,1)} %wo_any.1, s32[1,91]{1,0:T(1,128)} %bitcast.5), custom_call_target="tpu_custom_call" | custom-call | tf_op jit(solution)/shard_map/pallas_call | solution.py:333
  30.8 0.6 %copy.9 = bf16[1,8,1024]{2,1,0:T(8,128)(2,1)} copy(bf16[1,8,1024]{2,1,0:T(8,128)(2,1)S(1)} %bitcast.3) | data formatting | bytes 32768

commit v3 on v2

v3 whole, which is shorter than its diff:
```python
import functools
import math

import jax
import jax.numpy as jnp
from jax import lax
from jax.experimental import pallas as pl
from jax.experimental.pallas import tpu as pltpu
from jax.sharding import PartitionSpec as P

HEADS = 16
CORES = 2
LOWEST = -1e38
F32 = jnp.float32
BF16 = jnp.bfloat16
MESH = pl.DeviceIdType.MESH
NT = (((1,), (1,)), ((), ()))
TN = (((0,), (0,)), ((), ()))


def split(x):
    high = x.astype(BF16)
    return high, (x - high.astype(F32)).astype(BF16)


def dot(a, b):
    return jnp.dot(a, b, preferred_element_type=F32)


def pieces(lane):
    return (0, lane // 2), (lane // 2, lane // 2)


def flip(index, mask, size):
    bit = 1
    while bit < size:
        if mask & bit:
            index = index + bit - 2 * bit * (index // bit % 2)
        bit *= 2
    return index


def kernel(nx, ny, heads, tok_any, emb_any, qry_any, wk_any, wv_any, wo_any, slot_any, out,
           tok, emb, qry, wk, wo, slot, mixed, wbuf, wother, kq_mine, kq_in, kq_all, ex,
           stat, st_in, st2, st2_in, fexp, part, in1, p2, in2, o3, in3, early, spread_ex, tall,
           load_s, send_s, kq_r, z_r, w_r, tok_r, wo_r, st_r, st2_r, s1_r, s2_r, s3_r):
    _, slots, patches, width = tok.shape
    rows = width // ny
    na = ny // CORES
    group = patches // nx
    piece = rows // nx
    lane = width // CORES
    starts, sizes = pieces(lane)
    chunks = len(starts)
    wide = CORES * rows
    first_plane = na // CORES
    own = patches // (nx * ny)
    hdim = width // heads
    lheads = heads // CORES
    cheads = lheads // CORES
    held_slots = CORES * slots
    block_rows = held_slots * group
    scale = 1.0 / math.sqrt(hdim)
    i = lax.axis_index("vx")
    j = lax.axis_index("vy")
    a = j // CORES
    c = j % CORES
    partner = a * CORES + (1 - c)
    x_peers = [flip(i, d, nx) for d in reversed(range(1, nx))]
    mirror = x_peers[0]
    a_peers = [flip(a, d, na) for d in range(1, na)]
    vy_peers = [lax.rem(j + d, ny) for d in range(1, ny)]

    def remote(src, dst, rs, x, y):
        return pltpu.make_async_remote_copy(
            src_ref=src, dst_ref=dst, send_sem=send_s, recv_sem=rs,
            device_id=(x, y), device_id_type=MESH)

    sent = []

    def send(*args):
        copy = remote(*args)
        copy.start()
        sent.append(copy)

    def arrived(ref, rs):
        remote(ref, ref, rs, i, j).wait_recv()

    def cols(n):
        return slice(starts[n], starts[n] + sizes[n])

    def quarter(which, n):
        first = (n + which * (2 * CORES - 1 - 2 * n)) * sizes[n]
        return wv_any.at[:, pl.ds(pl.multiple_of(first, sizes[n]), sizes[n])]

    pairs = ((wk_any, wk), (qry_any, qry),
             (quarter(c, 0), wbuf.at[j, :, cols(0)]), (quarter(1 - c, 0), wother.at[:, cols(0)]),
             (quarter(c, 1), wbuf.at[j, :, cols(1)]), (quarter(1 - c, 1), wother.at[:, cols(1)]),
             (tok_any, tok.at[c]), (emb_any, emb), (slot_any, slot), (wo_any, wo.at[c]))
    loads = [pltpu.make_async_copy(src, dst, load_s.at[n]) for n, (src, dst) in enumerate(pairs)]
    for load in loads:
        load.start()

    barrier = pltpu.get_barrier_semaphore()
    for y in vy_peers:
        pl.semaphore_signal(barrier, inc=1, device_id=(i, y), device_id_type=MESH)
    for x in x_peers:
        pl.semaphore_signal(barrier, inc=1, device_id=(x, j), device_id_type=MESH)

    with jax.named_scope("A_load01"):
        loads[0].wait()
        loads[1].wait()
    head_row = lax.broadcasted_iota(jnp.int32, (heads, width), 0)
    head_col = lax.broadcasted_iota(jnp.int32, (heads, width), 1) // hdim
    qmat = jnp.where(head_row == head_col, jnp.broadcast_to(qry[...].astype(F32).reshape(1, width), (heads, width)), 0.0).astype(BF16)
    kq = lax.dot_general(qmat, wk[...], NT, preferred_element_type=F32)
    for d in range(CORES):
        for n in range(CORES):
            first = (n if d == 0 else 2 * CORES - 1 - n) * cheads
            kq_high, kq_low = split(kq[first:first + cheads])
            kq_mine[d, 0, n * cheads:(n + 1) * cheads] = kq_high
            kq_mine[d, 1, n * cheads:(n + 1) * cheads] = kq_low

    with jax.named_scope("B_barrier"):
        pl.semaphore_wait(barrier, (ny - 1) + (nx - 1))

    for y in vy_peers:
        send(kq_mine.at[y % CORES], kq_in.at[j], kq_r, i, y)

    def piece_rows(q):
        return pl.ds(pl.multiple_of(q * piece, piece), piece)

    with jax.named_scope("C_load23"):
        for load in loads[2:6]:
            load.wait()
    def along_z(q, n, x, sem):
        here = wbuf.at[j, piece_rows(q), cols(n)]
        send(here, here, sem, i, x * CORES + c)
        send(wother.at[piece_rows(q), cols(n)], here, sem, i, x * CORES + (1 - c))

    for n in range(chunks):
        for x in a_peers:
            along_z(i, n, x, z_r.at[n, a])
        if n == 0:
            along_z(mirror, n, a_peers[0], w_r.at[n, a])
        send(wother.at[:, cols(n)], wbuf.at[j, :, cols(n)], w_r.at[n, a], i, partner)
    with jax.named_scope("C_load4"):
        loads[6].wait()
    send(tok.at[c], tok.at[c], tok_r, i, partner)

    kq_in[j] = kq_mine[c]

    def pair_rows(x, q, n):
        return wbuf.at[pl.ds(pl.multiple_of(x * CORES, CORES), CORES), piece_rows(q), cols(n)]

    def share(n, x):
        here = pair_rows(x, i, n)
        arrived(here, z_r.at[n, x])
        for q in x_peers[1:] if n > 0 or x is a_peers[0] else x_peers:
            send(here, here, w_r.at[n, x], q, j)

    def complete(n, sources):
        for x in sources:
            if x is a:
                arrived(wbuf.at[partner, :, cols(n)], w_r.at[n, a])
            else:
                arrived(wbuf.at[pl.ds(pl.multiple_of(x * CORES, CORES), CORES), 0:(nx - 1) * piece, cols(n)], w_r.at[n, x])

    with jax.named_scope("D_loads"):
        for load in loads[7:]:
            load.wait()
    count = slot.shape[1]
    padded = -(-held_slots // 8) * 8
    ids = (i * ny + a * CORES) * slots + lax.broadcasted_iota(jnp.int32, (padded, count), 0)
    match = jnp.where(ids == jnp.broadcast_to(slot[...], (padded, count)), 1.0, 0.0)
    held = jnp.max(match, axis=1, keepdims=True)
    embed = dot(match.astype(BF16), emb[...])

    def mix(core):
        for s in range(slots):
            m = core * slots + s
            line = jnp.sum(jnp.where(lax.broadcasted_iota(jnp.int32, (padded, width), 0) == m, embed, 0.0), axis=0, keepdims=True)
            for g in range(nx):
                first = pl.multiple_of(g * block_rows + m * group, group)
                mixed[pl.ds(first, group), :] = (tok[core, s, g * group:(g + 1) * group, :].astype(F32) + line).astype(BF16)

    send(wo.at[c], wo.at[c], wo_r, i, partner)
    with jax.named_scope("E_mix"):
        mix(c)
    with jax.named_scope("F_share00"):
        share(0, a_peers[0])
    with jax.named_scope("G_tok"):
        arrived(tok.at[1 - c], tok_r)
    with jax.named_scope("G_mix2"):
        mix(1 - c)
    with jax.named_scope("G_share01"):
        for x in a_peers[1:-1]:
            share(0, x)
    for n in range(1, chunks):
        for x in a_peers:
            along_z(mirror, n, x, w_r.at[n, a])
    with jax.named_scope("J_share02"):
        share(0, a_peers[-1])
    with jax.named_scope("H_kq"):
        arrived(kq_in.at[0:ny - 1], kq_r)
    for y in range(ny):
        for d in range(2):
            kq_all[d * lheads:(d + 1) * lheads, y * rows:(y + 1) * rows] = kq_in[y, d]
    for g in range(nx):
        both = lax.dot_general(mixed[g * block_rows:(g + 1) * block_rows, :], kq_all[...], NT, preferred_element_type=F32)
        score = scale * (both[:, 0:lheads] + both[:, lheads:2 * lheads])
        top = jnp.full((group, lheads), LOWEST, F32)
        scores = []
        for s in range(held_slots):
            here = jnp.where(held[s:s + 1, :] > 0, score[s * group:(s + 1) * group], LOWEST)
            scores.append(here)
            top = jnp.maximum(top, here)
        total = jnp.zeros((group, lheads), F32)
        for s in range(held_slots):
            e = jnp.where(held[s:s + 1, :] > 0, jnp.exp(scores[s] - top), 0.0).astype(BF16)
            ex[g * block_rows + s * group:g * block_rows + (s + 1) * group, :] = e
            total += e.astype(F32)
        tall[g * group:(g + 1) * group, 0:lheads] = top
        tall[g * group:(g + 1) * group, lheads:2 * lheads] = total
    flat = tall[...].T
    for g in range(nx):
        for d in range(CORES):
            for k in range(2):
                first = k * lheads + d * cheads
                stat[g, d, k * cheads:(k + 1) * cheads] = flat[first:first + cheads, g * group:(g + 1) * group]

    for q in x_peers:
        for d in range(CORES):
            send(stat.at[q, d], st_in.at[i * CORES + c], st_r, q, a * CORES + d)
    send(stat.at[i, 1 - c], st_in.at[i * CORES + c], st_r, i, partner)
    st_in[i * CORES + c] = stat[i, c]

    with jax.named_scope("J_share1"):
        for n in range(1, chunks):
            for x in a_peers:
                share(n, x)

    def group_rows(g):
        return slice(g * block_rows, (g + 1) * block_rows)

    feature = lax.broadcasted_iota(jnp.int32, (lheads, lane), 1)
    spread = jnp.where(feature // hdim == lax.broadcasted_iota(jnp.int32, (lheads, lane), 0), 1.0, 0.0).astype(BF16)

    def plane_product(x, here, where):
        first = pl.multiple_of(x * wide, wide)
        weight = wbuf[pl.ds(pl.multiple_of(x * CORES, CORES), CORES), :, where].reshape(wide, -1)
        return dot(mixed[here, pl.ds(first, wide)], weight)

    def project_early(n, sources):
        for g in range(nx):
            here = group_rows(g)
            early[here, cols(n)] = sum(plane_product(x, here, cols(n)) for x in sources)

    def project_late(n, sources):
        for g in range(nx):
            here = group_rows(g)
            value = sum(plane_product(x, here, cols(n)) for x in sources)
            value = (value + early[here, cols(n)]) * spread_ex[here, cols(n)]
            part[n, g] = sum(value[s * group:(s + 1) * group] for s in range(held_slots)).astype(BF16)
        for q in x_peers:
            send(part.at[n, q], in1.at[i * CORES + c], s1_r, q, a * CORES + n)

        @pl.when(c == n)
        def _():
            in1[i * CORES + c] = part[n, i]

        @pl.when(c != n)
        def _():
            remote(part.at[n, i], in1.at[i * CORES + c], s1_r, i, partner).start()

    half_planes = first_plane // CORES
    targets = [(d, k) for d in range(CORES) for k in range(half_planes)]

    def target_of(d, k, core):
        return (c * half_planes + k if d == 0 else na - (c + 1) * half_planes + k) * CORES + core

    def scatter(d, k, core):
        return remote(p2.at[d * half_planes + k, core], in2.at[a], s2_r, i, target_of(d, k, core))

    def combine():
        arrived(in1.at[0:nx * CORES - 1], s1_r)
        for d in range(CORES):
            acc = sum(fexp[q, :, cols(d)] * in1[q * CORES + d].astype(F32) for q in range(nx))
            for k in range(half_planes):
                block = acc[:, k * wide:(k + 1) * wide]
                for core in range(CORES):
                    picked = [block[(x * CORES + core) * own:(x * CORES + core + 1) * own] for x in range(na)]
                    p2[d * half_planes + k, core] = jnp.concatenate(picked, axis=0).astype(BF16)
                    far = target_of(d, k, core) != j

                    @pl.when(far)
                    def _():
                        scatter(d, k, core).start()

    spread_ex[...] = dot(ex[...], spread)
    with jax.named_scope("K_complete0"):
        complete(0, [a] + a_peers[:-2])
    with jax.named_scope("K_early0"):
        project_early(0, [a] + a_peers[:-2])
    with jax.named_scope("L_complete0"):
        complete(0, a_peers[-2:])
    with jax.named_scope("M_project0"):
        project_late(0, a_peers[-2:])
    with jax.named_scope("K_st"):
        arrived(st_in.at[0:nx * CORES - 1], st_r)
    tops = [jnp.concatenate([st_in[q * CORES + d, 0:cheads] for d in range(CORES)], axis=0) for q in range(nx)]
    totals = [jnp.concatenate([st_in[q * CORES + d, cheads:2 * cheads] for d in range(CORES)], axis=0) for q in range(nx)]
    high = functools.reduce(jnp.maximum, tops)
    st2[0:lheads] = high
    st2[lheads:2 * lheads] = sum(
        jnp.exp(tops[q] - high) * totals[q] for q in range(nx))
    for x in a_peers:
        send(st2, st2_in.at[a], st2_r, i, x * CORES + c)
    st2_in[a] = st2[...]
    for n in range(1, chunks):
        with jax.named_scope("O_early1"):
            complete(n, [a])
            project_early(n, [a])
        with jax.named_scope("O_complete1"):
            complete(n, a_peers)
        with jax.named_scope("P_project1"):
            project_late(n, a_peers)
    with jax.named_scope("N_st2"):
        arrived(st2_in.at[0:na - 1], st2_r)
    highest = functools.reduce(jnp.maximum, [st2_in[p, 0:lheads] for p in range(na)])
    whole = sum(jnp.exp(st2_in[p, 0:lheads] - highest) * st2_in[p, lheads:2 * lheads] for p in range(na))
    for q in range(nx):
        f_high, f_low = split(jnp.exp(tops[q] - highest) / whole)
        fexp[q] = (lax.dot_general(f_high, spread, TN, preferred_element_type=F32)
                   + lax.dot_general(f_low, spread, TN, preferred_element_type=F32))

    with jax.named_scope("R_combine1"):
        combine()

    side = a // first_plane
    mine = (a + side * (na - 1 - 2 * a)) // half_planes == c

    @pl.when(mine)
    def _():
        in2[a] = p2[side * half_planes + lax.rem(a, half_planes), c]
        arrived(in2.at[0:na - 1], s2_r)

    @pl.when(jnp.logical_not(mine))
    def _():
        arrived(in2, s2_r)

    acc = sum(in2[x].astype(F32) for x in range(na))
    arrived(wo.at[1 - c], wo_r)
    result = dot(acc.astype(BF16), wo[...].reshape(wide, width)).astype(BF16)
    for x in range(na):
        o3[x] = result[x * own:(x + 1) * own]
    for x in a_peers:
        send(o3.at[x], in3.at[a], s3_r, i, x * CORES + c)
    final = o3[a].astype(F32)
    with jax.named_scope("T_in3"):
        arrived(in3.at[0:na - 1], s3_r)
    for x in a_peers:
        final += in3[x].astype(F32)
    out[...] = final.astype(BF16)
    with jax.named_scope("U_sends"):
        for copy in sent:
            copy.wait_send()
    for n in range(chunks):
        @pl.when(c != n)
        def _():
            remote(part.at[n, i], in1.at[i * CORES + c], s1_r, i, partner).wait_send()
    for d, k in targets:
        for core in range(CORES):
            @pl.when(target_of(d, k, core) != j)
            def _():
                scatter(d, k, core).wait_send()


def shards(tokens, var_embed, query, key_weight, value_weight, out_weight, var_slot):
    slots, batch, patches, width = tokens.shape
    nx, ny = lax.axis_size("vx"), lax.axis_size("vy")
    heads = HEADS
    patches = batch * patches
    rows, na, group, own = width // ny, ny // CORES, patches // nx, patches // (nx * ny)
    lane, lheads = width // CORES, heads // CORES
    chunks = len(pieces(lane)[0])
    held = CORES * slots * patches
    dma = pltpu.SemaphoreType.DMA
    vmem = pltpu.VMEM
    result = pl.pallas_call(
        functools.partial(kernel, nx, ny, heads),
        out_shape=vmem((own, width), BF16),
        in_specs=[pl.BlockSpec(memory_space=pl.ANY)] * 7,
        out_specs=pl.BlockSpec(memory_space=vmem),
        scratch_shapes=[
            vmem((CORES, slots, patches, width), BF16),
            vmem(var_embed.shape, BF16),
            vmem((width,), BF16),
            vmem((rows, width), BF16),
            vmem((CORES, rows, width), BF16),
            vmem((1, var_slot.shape[0]), jnp.int32),
            vmem((held, width), BF16),
            vmem((ny, rows, lane), BF16),
            vmem((rows, lane), BF16),
            vmem((CORES, 2, lheads, rows), BF16),
            vmem((ny, 2, lheads, rows), BF16),
            vmem((2 * lheads, width), BF16),
            vmem((held, lheads), BF16),
            vmem((nx, CORES, lheads, group), F32),
            vmem((nx * CORES, lheads, group), F32),
            vmem((2 * lheads, group), F32),
            vmem((na, 2 * lheads, group), F32),
            vmem((nx, group, lane), F32),
            vmem((chunks, nx, group, lane // chunks), BF16),
            vmem((nx * CORES, group, lane // chunks), BF16),
            vmem((na // CORES, CORES, na * own, CORES * rows), BF16),
            vmem((na, na * own, CORES * rows), BF16),
            vmem((na, own, width), BF16),
            vmem((na, own, width), BF16),
            vmem((held, lane), F32),
            vmem((held, lane), F32),
            vmem((patches, 128), F32),
            dma((10,)), dma, dma, dma((chunks, na)), dma((chunks, na)), dma, dma, dma, dma,
            dma, dma, dma,
        ],
        compiler_params=pltpu.CompilerParams(
            collective_id=0, has_side_effects=True, vmem_limit_bytes=56 * 1024 * 1024),
    )(
        tokens.reshape(slots, patches, width), var_embed, query,
        key_weight, value_weight, out_weight, var_slot.reshape(1, -1),
    )
    return result.reshape(batch, -1, width)


def solution(mesh):
    placed = (
        P(("vx", "vy"), None, None, None),
        P(),
        P(),
        P("vy", None),
        P("vy", None),
        P("vy", None),
        P(),
    )
    return jax.shard_map(
        shards, mesh=mesh, in_specs=placed, out_specs=P(None, ("vx", "vy"), None), check_vma=False
    )
```

time: 31.6 us -> 29.4 us (0.930)
  Pallas kernels: 30.8 us -> 28.7 us
    pallas_call x1, Pallas kernels: 30.8 us -> 28.7 us  [shards(): pl.pallas_call(functools.partial(kernel, nx, ny, heads), out_shape=vmem((...]
where the time goes in v3:
time: 29.4 us; the launch traced here: 29.3 us
  Pallas kernels  28.7 us (98%)
  local copies, waits for them, and re-layouts  0.61 us (2%)
    pallas_call x1, Pallas kernels, shards(): pl.pallas_call(functools.partial(kernel, nx, ny, heads), out_shape=vmem((...  28.7 us
    unnamed x1, local copies, waits for them, and re-layouts  0.61 us

profile of v3, /device:TPU:0, one launch (start us, length us, event | category | flops | bytes accessed | tf_op | source)
XLA Modules:
  0.0 29.3 jit_solution(13435716915108957280)
XLA Ops:
  0.0 28.7 %shard_map.73 = bf16[8,1024]{1,0:T(8,128)(2,1)S(1)} custom-call(bf16[3,256,1024]{2,1,0:T(8,128)(2,1)} %bitcast.4, bf16[91,1024]{1,0:T(8,128)(2,1)} %emb_any.1, bf16[1024]{0:T(1024)(128)(2,1)} %qry_any.1, bf16[128,1024]{1,0:T(8,128)(2,1)} %wk_any.1, bf16[128,1024]{1,0:T(8,128)(2,1)} %wv_any.1, bf16[128,1024]{1,0:T(8,128)(2,1)} %wo_any.1, s32[1,91]{1,0:T(1,128)} %bitcast.5), custom_call_target="tpu_custom_call" | custom-call | tf_op jit(solution)/shard_map/pallas_call | solution.py:390
  28.7 0.6 %copy.9 = bf16[1,8,1024]{2,1,0:T(8,128)(2,1)} copy(bf16[1,8,1024]{2,1,0:T(8,128)(2,1)S(1)} %bitcast.3) | data formatting | bytes 32768

commit v4 on v3

--- a/solution.py
+++ b/solution.py
@@ -42,7 +42,7 @@
 
 def kernel(nx, ny, heads, tok_any, emb_any, qry_any, wk_any, wv_any, wo_any, slot_any, out,
            tok, emb, qry, wk, wo, slot, mixed, wbuf, wother, kq_mine, kq_in, kq_all, ex,
-           stat, st_in, st2, st2_in, fexp, part, in1, p2, in2, o3, in3, early, spread_ex, tall,
+           stat, st_in, st2, st2_in, fexp, part, in1, p2, in2, o3, in3, early, spread_ex, tall, fz,
            load_s, send_s, kq_r, z_r, w_r, tok_r, wo_r, st_r, st2_r, s1_r, s2_r, s3_r):
     _, slots, patches, width = tok.shape
     rows = width // ny
@@ -86,6 +86,12 @@
     def arrived(ref, rs):
         remote(ref, ref, rs, i, j).wait_recv()
 
+    barrier = pltpu.get_barrier_semaphore()
+    for y in vy_peers:
+        pl.semaphore_signal(barrier, inc=1, device_id=(i, y), device_id_type=MESH)
+    for x in x_peers:
+        pl.semaphore_signal(barrier, inc=1, device_id=(x, j), device_id_type=MESH)
+
     def cols(n):
         return slice(starts[n], starts[n] + sizes[n])
 
@@ -100,12 +106,6 @@
     loads = [pltpu.make_async_copy(src, dst, load_s.at[n]) for n, (src, dst) in enumerate(pairs)]
     for load in loads:
         load.start()
-
-    barrier = pltpu.get_barrier_semaphore()
-    for y in vy_peers:
-        pl.semaphore_signal(barrier, inc=1, device_id=(i, y), device_id_type=MESH)
-    for x in x_peers:
-        pl.semaphore_signal(barrier, inc=1, device_id=(x, j), device_id_type=MESH)
 
     with jax.named_scope("A_load01"):
         loads[0].wait()
@@ -184,7 +184,12 @@
                 first = pl.multiple_of(g * block_rows + m * group, group)
                 mixed[pl.ds(first, group), :] = (tok[core, s, g * group:(g + 1) * group, :].astype(F32) + line).astype(BF16)
 
-    send(wo.at[c], wo.at[c], wo_r, i, partner)
+    lend = remote(wo.at[0], wo.at[0], wo_r, i, partner)
+
+    @pl.when(c == 0)
+    def _():
+        lend.start()
+
     with jax.named_scope("E_mix"):
         mix(c)
     with jax.named_scope("F_share00"):
@@ -257,13 +262,16 @@
             early[here, cols(n)] = sum(plane_product(x, here, cols(n)) for x in sources)
 
     def project_late(n, sources):
-        for g in range(nx):
-            here = group_rows(g)
-            value = sum(plane_product(x, here, cols(n)) for x in sources)
-            value = (value + early[here, cols(n)]) * spread_ex[here, cols(n)]
-            part[n, g] = sum(value[s * group:(s + 1) * group] for s in range(held_slots)).astype(BF16)
-        for q in x_peers:
-            send(part.at[n, q], in1.at[i * CORES + c], s1_r, q, a * CORES + n)
+        near = nx // 2 - 1
+        for batch in (x_peers[:near] + [i], x_peers[near:]):
+            for g in batch:
+                here = pl.ds(pl.multiple_of(g * block_rows, block_rows), block_rows)
+                value = sum(plane_product(x, here, cols(n)) for x in sources)
+                value = (value + early[here, cols(n)]) * spread_ex[here, cols(n)]
+                part[n, g] = sum(value[s * group:(s + 1) * group] for s in range(held_slots)).astype(BF16)
+            for g in batch:
+                if g is not i:
+                    send(part.at[n, g], in1.at[i * CORES + c], s1_r, g, a * CORES + n)
 
         @pl.when(c == n)
         def _():
@@ -276,26 +284,25 @@
     half_planes = first_plane // CORES
     targets = [(d, k) for d in range(CORES) for k in range(half_planes)]
 
-    def target_of(d, k, core):
-        return (c * half_planes + k if d == 0 else na - (c + 1) * half_planes + k) * CORES + core
-
-    def scatter(d, k, core):
-        return remote(p2.at[d * half_planes + k, core], in2.at[a], s2_r, i, target_of(d, k, core))
+    def target_of(d, k):
+        return (c * half_planes + k if d == 0 else na - (c + 1) * half_planes + k) * CORES + CORES - 1
+
+    def scatter(d, k):
+        return remote(p2.at[d * half_planes + k], in2.at[a], s2_r, i, target_of(d, k))
+
+    def scatter_stats(d, k):
+        return remote(st2.at[d], st2_in.at[a], st2_r, i, target_of(d, k))
 
     def combine():
         arrived(in1.at[0:nx * CORES - 1], s1_r)
         for d in range(CORES):
             acc = sum(fexp[q, :, cols(d)] * in1[q * CORES + d].astype(F32) for q in range(nx))
             for k in range(half_planes):
-                block = acc[:, k * wide:(k + 1) * wide]
-                for core in range(CORES):
-                    picked = [block[(x * CORES + core) * own:(x * CORES + core + 1) * own] for x in range(na)]
-                    p2[d * half_planes + k, core] = jnp.concatenate(picked, axis=0).astype(BF16)
-                    far = target_of(d, k, core) != j
-
-                    @pl.when(far)
-                    def _():
-                        scatter(d, k, core).start()
+                p2[d * half_planes + k] = acc[:, k * wide:(k + 1) * wide].astype(BF16)
+
+                @pl.when(target_of(d, k) != j)
+                def _():
+                    scatter(d, k).start()
 
     spread_ex[...] = dot(ex[...], spread)
     with jax.named_scope("K_complete0"):
@@ -311,12 +318,21 @@
     tops = [jnp.concatenate([st_in[q * CORES + d, 0:cheads] for d in range(CORES)], axis=0) for q in range(nx)]
     totals = [jnp.concatenate([st_in[q * CORES + d, cheads:2 * cheads] for d in range(CORES)], axis=0) for q in range(nx)]
     high = functools.reduce(jnp.maximum, tops)
-    st2[0:lheads] = high
-    st2[lheads:2 * lheads] = sum(
-        jnp.exp(tops[q] - high) * totals[q] for q in range(nx))
-    for x in a_peers:
-        send(st2, st2_in.at[a], st2_r, i, x * CORES + c)
-    st2_in[a] = st2[...]
+    below = [jnp.exp(tops[q] - high) for q in range(nx)]
+    total = sum(below[q] * totals[q] for q in range(nx))
+    for d in range(CORES):
+        st2[d, 0:cheads] = high[d * cheads:(d + 1) * cheads]
+        st2[d, cheads:lheads] = total[d * cheads:(d + 1) * cheads]
+    for d, k in targets:
+        @pl.when(target_of(d, k) != j)
+        def _():
+            scatter_stats(d, k).start()
+
+    for q in range(nx):
+        f_high, f_low = split(below[q])
+        fexp[q] = (lax.dot_general(f_high, spread, TN, preferred_element_type=F32)
+                   + lax.dot_general(f_low, spread, TN, preferred_element_type=F32))
+
     for n in range(1, chunks):
         with jax.named_scope("O_early1"):
             complete(n, [a])
@@ -325,42 +341,63 @@
             complete(n, a_peers)
         with jax.named_scope("P_project1"):
             project_late(n, a_peers)
-    with jax.named_scope("N_st2"):
-        arrived(st2_in.at[0:na - 1], st2_r)
-    highest = functools.reduce(jnp.maximum, [st2_in[p, 0:lheads] for p in range(na)])
-    whole = sum(jnp.exp(st2_in[p, 0:lheads] - highest) * st2_in[p, lheads:2 * lheads] for p in range(na))
-    for q in range(nx):
-        f_high, f_low = split(jnp.exp(tops[q] - highest) / whole)
-        fexp[q] = (lax.dot_general(f_high, spread, TN, preferred_element_type=F32)
-                   + lax.dot_general(f_low, spread, TN, preferred_element_type=F32))
-
     with jax.named_scope("R_combine1"):
         combine()
 
     side = a // first_plane
-    mine = (a + side * (na - 1 - 2 * a)) // half_planes == c
-
-    @pl.when(mine)
+    spot = lax.rem(a, half_planes)
+    mine = (a + side * (na - 1 - 2 * a)) // half_planes == CORES - 1
+
+    @pl.when(c == CORES - 1)
     def _():
-        in2[a] = p2[side * half_planes + lax.rem(a, half_planes), c]
-        arrived(in2.at[0:na - 1], s2_r)
-
-    @pl.when(jnp.logical_not(mine))
+        @pl.when(mine)
+        def _():
+            st2_in[a] = st2[side]
+            in2[a] = p2[side * half_planes + spot]
+            arrived(st2_in.at[0:na - 1], st2_r)
+
+        @pl.when(jnp.logical_not(mine))
+        def _():
+            arrived(st2_in, st2_r)
+
+        highest = functools.reduce(jnp.maximum, [st2_in[p, 0:cheads] for p in range(na)])
+        lower = [jnp.exp(st2_in[p, 0:cheads] - highest) for p in range(na)]
+        whole = sum(lower[p] * st2_in[p, cheads:lheads] for p in range(na))
+        wanted = (spot * wide + lax.broadcasted_iota(jnp.int32, (cheads, wide), 1)) // hdim
+        widen = jnp.where(wanted == lax.broadcasted_iota(jnp.int32, (cheads, wide), 0), 1.0, 0.0).astype(BF16)
+        for p in range(na):
+            f_high, f_low = split(lower[p] / whole)
+            fz[p] = (lax.dot_general(f_high, widen, TN, preferred_element_type=F32)
+                     + lax.dot_general(f_low, widen, TN, preferred_element_type=F32))
+        arrived(wo.at[0], wo_r)
+
+        with jax.named_scope("S_in2"):
+            @pl.when(mine)
+            def _():
+                arrived(in2.at[0:na - 1], s2_r)
+
+            @pl.when(jnp.logical_not(mine))
+            def _():
+                arrived(in2, s2_r)
+
+        acc = sum(fz[p] * in2[p].astype(F32) for p in range(na))
+        result = dot(acc.astype(BF16), wo[...].reshape(wide, width)).astype(BF16)
+        for y in range(ny):
+            o3[y] = result[y * own:(y + 1) * own]
+        for x in reversed(a_peers):
+            for d in range(CORES):
+                remote(o3.at[x * CORES + d], in3.at[a], s3_r, i, x * CORES + d).start()
+        remote(o3.at[partner], in3.at[a], s3_r, i, partner).start()
+        in3[a] = o3[j]
+        with jax.named_scope("T_in3n"):
+            arrived(in3.at[0:na - 1], s3_r)
+
+    @pl.when(c != CORES - 1)
     def _():
-        arrived(in2, s2_r)
-
-    acc = sum(in2[x].astype(F32) for x in range(na))
-    arrived(wo.at[1 - c], wo_r)
-    result = dot(acc.astype(BF16), wo[...].reshape(wide, width)).astype(BF16)
-    for x in range(na):
-        o3[x] = result[x * own:(x + 1) * own]
-    for x in a_peers:
-        send(o3.at[x], in3.at[a], s3_r, i, x * CORES + c)
-    final = o3[a].astype(F32)
-    with jax.named_scope("T_in3"):
-        arrived(in3.at[0:na - 1], s3_r)
-    for x in a_peers:
-        final += in3[x].astype(F32)
+        with jax.named_scope("T_in3s"):
+            arrived(in3, s3_r)
+
+    final = sum(in3[x].astype(F32) for x in range(na))
     out[...] = final.astype(BF16)
     with jax.named_scope("U_sends"):
         for copy in sent:
@@ -370,10 +407,19 @@
         def _():
             remote(part.at[n, i], in1.at[i * CORES + c], s1_r, i, partner).wait_send()
     for d, k in targets:
-        for core in range(CORES):
-            @pl.when(target_of(d, k, core) != j)
-            def _():
-                scatter(d, k, core).wait_send()
+        @pl.when(target_of(d, k) != j)
+        def _():
+            scatter(d, k).wait_send()
+            scatter_stats(d, k).wait_send()
+
+    @pl.when(c == 0)
+    def _():
+        lend.wait_send()
+
+    @pl.when(c == CORES - 1)
+    def _():
+        for y in vy_peers:
+            remote(o3.at[y], in3.at[a], s3_r, i, y).wait_send()
 
 
 def shards(tokens, var_embed, query, key_weight, value_weight, out_weight, var_slot):
@@ -408,18 +454,19 @@
             vmem((held, lheads), BF16),
             vmem((nx, CORES, lheads, group), F32),
             vmem((nx * CORES, lheads, group), F32),
-            vmem((2 * lheads, group), F32),
-            vmem((na, 2 * lheads, group), F32),
+            vmem((CORES, lheads, group), F32),
+            vmem((na, lheads, group), F32),
             vmem((nx, group, lane), F32),
             vmem((chunks, nx, group, lane // chunks), BF16),
             vmem((nx * CORES, group, lane // chunks), BF16),
-            vmem((na // CORES, CORES, na * own, CORES * rows), BF16),
-            vmem((na, na * own, CORES * rows), BF16),
-            vmem((na, own, width), BF16),
+            vmem((na // CORES, group, CORES * rows), BF16),
+            vmem((na, group, CORES * rows), BF16),
+            vmem((ny, own, width), BF16),
             vmem((na, own, width), BF16),
             vmem((held, lane), F32),
             vmem((held, lane), F32),
             vmem((patches, 128), F32),
+            vmem((na, group, CORES * rows), F32),
             dma((10,)), dma, dma, dma((chunks, na)), dma((chunks, na)), dma, dma, dma, dma,
             dma, dma, dma,
         ],

time: 29.4 us -> 28.6 us (0.973)
  Pallas kernels: 28.7 us -> 27.8 us
    pallas_call x1, Pallas kernels: 28.7 us -> 27.8 us  [shards(): pl.pallas_call(functools.partial(kernel, nx, ny, heads), out_shape=vmem((...]
where the time goes in v4:
time: 28.6 us; the launch traced here: 28.5 us
  Pallas kernels  27.8 us (97%)
  local copies, waits for them, and re-layouts  0.61 us (2%)
    pallas_call x1, Pallas kernels, shards(): pl.pallas_call(functools.partial(kernel, nx, ny, heads), out_shape=vmem((...  27.8 us
    unnamed x1, local copies, waits for them, and re-layouts  0.61 us

profile of v4, /device:TPU:0, one launch (start us, length us, event | category | flops | bytes accessed | tf_op | source)
XLA Modules:
  0.0 28.5 jit_solution(7281051349369040952)
XLA Ops:
  0.0 27.8 %shard_map.73 = bf16[8,1024]{1,0:T(8,128)(2,1)S(1)} custom-call(bf16[3,256,1024]{2,1,0:T(8,128)(2,1)} %bitcast.4, bf16[91,1024]{1,0:T(8,128)(2,1)} %emb_any.1, bf16[1024]{0:T(1024)(128)(2,1)} %qry_any.1, bf16[128,1024]{1,0:T(8,128)(2,1)} %wk_any.1, bf16[128,1024]{1,0:T(8,128)(2,1)} %wv_any.1, bf16[128,1024]{1,0:T(8,128)(2,1)} %wo_any.1, s32[1,91]{1,0:T(1,128)} %bitcast.5), custom_call_target="tpu_custom_call" | custom-call | tf_op jit(solution)/shard_map/pallas_call | solution.py:436
  27.9 0.6 %copy.9 = bf16[1,8,1024]{2,1,0:T(8,128)(2,1)} copy(bf16[1,8,1024]{2,1,0:T(8,128)(2,1)S(1)} %bitcast.3) | data formatting | bytes 32768

commit v5 on v4

--- a/solution.py
+++ b/solution.py
@@ -41,7 +41,7 @@
 
 
 def kernel(nx, ny, heads, tok_any, emb_any, qry_any, wk_any, wv_any, wo_any, slot_any, out,
-           tok, emb, qry, wk, wo, slot, mixed, wbuf, wother, kq_mine, kq_in, kq_all, ex,
+           tok, emb, qry, wk, wo, slot, mixed, wbuf, wsrc, kq_mine, kq_in, kq_all, ex,
            stat, st_in, st2, st2_in, fexp, part, in1, p2, in2, o3, in3, early, spread_ex, tall, fz,
            load_s, send_s, kq_r, z_r, w_r, tok_r, wo_r, st_r, st2_r, s1_r, s2_r, s3_r):
     _, slots, patches, width = tok.shape
@@ -96,12 +96,15 @@
         return slice(starts[n], starts[n] + sizes[n])
 
     def quarter(which, n):
-        first = (n + which * (2 * CORES - 1 - 2 * n)) * sizes[n]
+        first = (which + CORES * (1 - n)) * sizes[n]
+        if isinstance(which, int):
+            return wv_any.at[:, first:first + sizes[n]]
         return wv_any.at[:, pl.ds(pl.multiple_of(first, sizes[n]), sizes[n])]
 
     pairs = ((wk_any, wk), (qry_any, qry),
-             (quarter(c, 0), wbuf.at[j, :, cols(0)]), (quarter(1 - c, 0), wother.at[:, cols(0)]),
-             (quarter(c, 1), wbuf.at[j, :, cols(1)]), (quarter(1 - c, 1), wother.at[:, cols(1)]),
+             (quarter(0, 0), wsrc.at[0, :, cols(0)]), (quarter(1, 0), wsrc.at[1, :, cols(0)]),
+             (quarter(0, 1), wsrc.at[0, :, cols(1)]), (quarter(1, 1), wsrc.at[1, :, cols(1)]),
+             (quarter(c, 0), wbuf.at[j, :, cols(0)]), (quarter(c, 1), wbuf.at[j, :, cols(1)]),
              (tok_any, tok.at[c]), (emb_any, emb), (slot_any, slot), (wo_any, wo.at[c]))
     loads = [pltpu.make_async_copy(src, dst, load_s.at[n]) for n, (src, dst) in enumerate(pairs)]
     for load in loads:
@@ -116,7 +119,7 @@
     kq = lax.dot_general(qmat, wk[...], NT, preferred_element_type=F32)
     for d in range(CORES):
         for n in range(CORES):
-            first = (n if d == 0 else 2 * CORES - 1 - n) * cheads
+            first = (d + CORES * (1 - n)) * cheads
             kq_high, kq_low = split(kq[first:first + cheads])
             kq_mine[d, 0, n * cheads:(n + 1) * cheads] = kq_high
             kq_mine[d, 1, n * cheads:(n + 1) * cheads] = kq_low
@@ -124,8 +127,6 @@
     with jax.named_scope("B_barrier"):
         pl.semaphore_wait(barrier, (ny - 1) + (nx - 1))
 
-    for y in vy_peers:
-        send(kq_mine.at[y % CORES], kq_in.at[j], kq_r, i, y)
 
     def piece_rows(q):
         return pl.ds(pl.multiple_of(q * piece, piece), piece)
@@ -134,18 +135,20 @@
         for load in loads[2:6]:
             load.wait()
     def along_z(q, n, x, sem):
-        here = wbuf.at[j, piece_rows(q), cols(n)]
-        send(here, here, sem, i, x * CORES + c)
-        send(wother.at[piece_rows(q), cols(n)], here, sem, i, x * CORES + (1 - c))
+        for d in range(CORES):
+            send(wsrc.at[d, piece_rows(q), cols(n)], wbuf.at[j, piece_rows(q), cols(n)], sem, i, x * CORES + d)
 
     for n in range(chunks):
         for x in a_peers:
             along_z(i, n, x, z_r.at[n, a])
+            if n == 0 and x is a_peers[0]:
+                for y in vy_peers:
+                    send(kq_mine.at[y % CORES], kq_in.at[j], kq_r, i, y)
         if n == 0:
             along_z(mirror, n, a_peers[0], w_r.at[n, a])
-        send(wother.at[:, cols(n)], wbuf.at[j, :, cols(n)], w_r.at[n, a], i, partner)
+        send(wsrc.at[1 - c, :, cols(n)], wbuf.at[j, :, cols(n)], w_r.at[n, a], i, partner)
     with jax.named_scope("C_load4"):
-        loads[6].wait()
+        loads[8].wait()
     send(tok.at[c], tok.at[c], tok_r, i, partner)
 
     kq_in[j] = kq_mine[c]
@@ -167,7 +170,7 @@
                 arrived(wbuf.at[pl.ds(pl.multiple_of(x * CORES, CORES), CORES), 0:(nx - 1) * piece, cols(n)], w_r.at[n, x])
 
     with jax.named_scope("D_loads"):
-        for load in loads[7:]:
+        for load in loads[6:8] + loads[9:]:
             load.wait()
     count = slot.shape[1]
     padded = -(-held_slots // 8) * 8
@@ -229,16 +232,21 @@
         tall[g * group:(g + 1) * group, lheads:2 * lheads] = total
     flat = tall[...].T
     for g in range(nx):
-        for d in range(CORES):
-            for k in range(2):
-                first = k * lheads + d * cheads
-                stat[g, d, k * cheads:(k + 1) * cheads] = flat[first:first + cheads, g * group:(g + 1) * group]
+        stat[g] = flat[0:2 * lheads, g * group:(g + 1) * group]
+
+    def lend_stats():
+        return remote(stat.at[i], st_in.at[i * CORES], st_r, i, partner)
 
     for q in x_peers:
-        for d in range(CORES):
-            send(stat.at[q, d], st_in.at[i * CORES + c], st_r, q, a * CORES + d)
-    send(stat.at[i, 1 - c], st_in.at[i * CORES + c], st_r, i, partner)
-    st_in[i * CORES + c] = stat[i, c]
+        send(stat.at[q], st_in.at[i * CORES + c], st_r, q, a * CORES + CORES - 1)
+
+    @pl.when(c == 0)
+    def _():
+        lend_stats().start()
+
+    @pl.when(c == CORES - 1)
+    def _():
+        st_in[i * CORES + c] = stat[i]
 
     with jax.named_scope("J_share1"):
         for n in range(1, chunks):
@@ -256,53 +264,82 @@
         weight = wbuf[pl.ds(pl.multiple_of(x * CORES, CORES), CORES), :, where].reshape(wide, -1)
         return dot(mixed[here, pl.ds(first, wide)], weight)
 
-    def project_early(n, sources):
+    def project_early(n, sources, more=False):
         for g in range(nx):
             here = group_rows(g)
-            early[here, cols(n)] = sum(plane_product(x, here, cols(n)) for x in sources)
+            value = sum(plane_product(x, here, cols(n)) for x in sources)
+            early[here, cols(n)] = value + early[here, cols(n)] if more else value
+
+    def give(n, g):
+        return remote(part.at[n, g], in1.at[n, i * CORES + c], s1_r.at[n], g, a * CORES + CORES - 1)
 
     def project_late(n, sources):
-        near = nx // 2 - 1
-        for batch in (x_peers[:near] + [i], x_peers[near:]):
+        for batch in (range(2), range(2, nx)):
             for g in batch:
-                here = pl.ds(pl.multiple_of(g * block_rows, block_rows), block_rows)
+                here = group_rows(g)
                 value = sum(plane_product(x, here, cols(n)) for x in sources)
                 value = (value + early[here, cols(n)]) * spread_ex[here, cols(n)]
                 part[n, g] = sum(value[s * group:(s + 1) * group] for s in range(held_slots)).astype(BF16)
             for g in batch:
-                if g is not i:
-                    send(part.at[n, g], in1.at[i * CORES + c], s1_r, g, a * CORES + n)
-
-        @pl.when(c == n)
+                @pl.when(i != g)
+                def _():
+                    give(n, g).start()
+
+        for q in x_peers:
+            sent.append(give(n, q))
+
+        @pl.when(c == CORES - 1)
         def _():
-            in1[i * CORES + c] = part[n, i]
-
-        @pl.when(c != n)
+            in1[n, i * CORES + c] = part[n, i]
+
+        @pl.when(c == 0)
         def _():
-            remote(part.at[n, i], in1.at[i * CORES + c], s1_r, i, partner).start()
+            give(n, i).start()
 
     half_planes = first_plane // CORES
-    targets = [(d, k) for d in range(CORES) for k in range(half_planes)]
-
-    def target_of(d, k):
-        return (c * half_planes + k if d == 0 else na - (c + 1) * half_planes + k) * CORES + CORES - 1
-
-    def scatter(d, k):
-        return remote(p2.at[d * half_planes + k], in2.at[a], s2_r, i, target_of(d, k))
-
-    def scatter_stats(d, k):
-        return remote(st2.at[d], st2_in.at[a], st2_r, i, target_of(d, k))
-
-    def combine():
-        arrived(in1.at[0:nx * CORES - 1], s1_r)
+    targets = [(d, k) for d in reversed(range(CORES)) for k in range(half_planes)]
+
+    def target_of(d, k, n):
+        return ((d + CORES * (1 - n)) * half_planes + k) * CORES + CORES - 1
+
+    def scatter(d, k, n):
+        return remote(p2.at[n, d * half_planes + k], in2.at[a], s2_r, i, target_of(d, k, n))
+
+    def scatter_stats(d, k, n):
+        return remote(st2.at[d, n], st2_in.at[a], st2_r, i, target_of(d, k, n))
+
+    def plane_stats():
+        with jax.named_scope("K_st"):
+            arrived(st_in.at[0:nx * CORES - 1], st_r)
         for d in range(CORES):
-            acc = sum(fexp[q, :, cols(d)] * in1[q * CORES + d].astype(F32) for q in range(nx))
+            tops = [st_in[q * CORES + d, 0:lheads] for q in range(nx)]
+            high = functools.reduce(jnp.maximum, tops)
+            below = [jnp.exp(top - high) for top in tops]
+            total = sum(below[q] * st_in[q * CORES + d, lheads:2 * lheads] for q in range(nx))
+            for n in range(chunks):
+                heads_n = slice(n * cheads, (n + 1) * cheads)
+                st2[d, n, 0:cheads] = high[heads_n]
+                st2[d, n, cheads:lheads] = total[heads_n]
+            for q in range(nx):
+                f_high, f_low = split(below[q])
+                fexp[q * CORES + d] = (lax.dot_general(f_high, spread, TN, preferred_element_type=F32)
+                                       + lax.dot_general(f_low, spread, TN, preferred_element_type=F32))
+        for n in range(chunks):
+            for d, k in targets:
+                @pl.when(target_of(d, k, n) != j)
+                def _():
+                    scatter_stats(d, k, n).start()
+
+    def combine(n):
+        arrived(in1.at[n, 0:nx * CORES - 1], s1_r.at[n])
+        for d in reversed(range(CORES)):
+            acc = sum(fexp[q * CORES + d, :, cols(n)] * in1[n, q * CORES + d].astype(F32) for q in range(nx))
             for k in range(half_planes):
-                p2[d * half_planes + k] = acc[:, k * wide:(k + 1) * wide].astype(BF16)
-
-                @pl.when(target_of(d, k) != j)
+                p2[n, d * half_planes + k] = acc[:, k * wide:(k + 1) * wide].astype(BF16)
+
+                @pl.when(target_of(d, k, n) != j)
                 def _():
-                    scatter(d, k).start()
+                    scatter(d, k, n).start()
 
     spread_ex[...] = dot(ex[...], spread)
     with jax.named_scope("K_complete0"):
@@ -313,52 +350,41 @@
         complete(0, a_peers[-2:])
     with jax.named_scope("M_project0"):
         project_late(0, a_peers[-2:])
-    with jax.named_scope("K_st"):
-        arrived(st_in.at[0:nx * CORES - 1], st_r)
-    tops = [jnp.concatenate([st_in[q * CORES + d, 0:cheads] for d in range(CORES)], axis=0) for q in range(nx)]
-    totals = [jnp.concatenate([st_in[q * CORES + d, cheads:2 * cheads] for d in range(CORES)], axis=0) for q in range(nx)]
-    high = functools.reduce(jnp.maximum, tops)
-    below = [jnp.exp(tops[q] - high) for q in range(nx)]
-    total = sum(below[q] * totals[q] for q in range(nx))
-    for d in range(CORES):
-        st2[d, 0:cheads] = high[d * cheads:(d + 1) * cheads]
-        st2[d, cheads:lheads] = total[d * cheads:(d + 1) * cheads]
-    for d, k in targets:
-        @pl.when(target_of(d, k) != j)
-        def _():
-            scatter_stats(d, k).start()
-
-    for q in range(nx):
-        f_high, f_low = split(below[q])
-        fexp[q] = (lax.dot_general(f_high, spread, TN, preferred_element_type=F32)
-                   + lax.dot_general(f_low, spread, TN, preferred_element_type=F32))
+    @pl.when(c == CORES - 1)
+    def _():
+        plane_stats()
 
     for n in range(1, chunks):
         with jax.named_scope("O_early1"):
             complete(n, [a])
             project_early(n, [a])
         with jax.named_scope("O_complete1"):
-            complete(n, a_peers)
+            complete(n, a_peers[:-1])
+        with jax.named_scope("O_early2"):
+            project_early(n, a_peers[:-1], True)
+        with jax.named_scope("O_complete2"):
+            complete(n, a_peers[-1:])
         with jax.named_scope("P_project1"):
-            project_late(n, a_peers)
-    with jax.named_scope("R_combine1"):
-        combine()
-
+            project_late(n, a_peers[-1:])
+    block = a // half_planes
+    spot = lax.rem(a, half_planes)
+    my_chunk = 1 - block // CORES
+    my_lane = lax.rem(block, CORES)
     side = a // first_plane
-    spot = lax.rem(a, half_planes)
-    mine = (a + side * (na - 1 - 2 * a)) // half_planes == CORES - 1
+    fold = a + side * (na - 1 - 2 * a)
+    steps = [na - 1 - k - (k + fold + 1) // na for k in range(na - 1)]
+    far_first = [p + side * (na - 1 - 2 * p) for p in steps]
+    turned = (1 - side) * ((a + na - 1) // na)
+    root_first = [far_first[k] + turned * (far_first[k - 1] - far_first[k]) for k in range(na - 1)]
 
     @pl.when(c == CORES - 1)
     def _():
-        @pl.when(mine)
-        def _():
-            st2_in[a] = st2[side]
-            in2[a] = p2[side * half_planes + spot]
-            arrived(st2_in.at[0:na - 1], st2_r)
-
-        @pl.when(jnp.logical_not(mine))
-        def _():
-            arrived(st2_in, st2_r)
+        for n in range(chunks):
+            with jax.named_scope(f"R_combine{n}"):
+                combine(n)
+        st2_in[a] = st2[my_lane, my_chunk]
+        in2[a] = p2[my_chunk, my_lane * half_planes + spot]
+        arrived(st2_in.at[0:na - 1], st2_r)
 
         highest = functools.reduce(jnp.maximum, [st2_in[p, 0:cheads] for p in range(na)])
         lower = [jnp.exp(st2_in[p, 0:cheads] - highest) for p in range(na)]
@@ -372,19 +398,13 @@
         arrived(wo.at[0], wo_r)
 
         with jax.named_scope("S_in2"):
-            @pl.when(mine)
-            def _():
-                arrived(in2.at[0:na - 1], s2_r)
-
-            @pl.when(jnp.logical_not(mine))
-            def _():
-                arrived(in2, s2_r)
+            arrived(in2.at[0:na - 1], s2_r)
 
         acc = sum(fz[p] * in2[p].astype(F32) for p in range(na))
         result = dot(acc.astype(BF16), wo[...].reshape(wide, width)).astype(BF16)
         for y in range(ny):
             o3[y] = result[y * own:(y + 1) * own]
-        for x in reversed(a_peers):
+        for x in root_first:
             for d in range(CORES):
                 remote(o3.at[x * CORES + d], in3.at[a], s3_r, i, x * CORES + d).start()
         remote(o3.at[partner], in3.at[a], s3_r, i, partner).start()
@@ -402,22 +422,21 @@
     with jax.named_scope("U_sends"):
         for copy in sent:
             copy.wait_send()
-    for n in range(chunks):
-        @pl.when(c != n)
-        def _():
-            remote(part.at[n, i], in1.at[i * CORES + c], s1_r, i, partner).wait_send()
-    for d, k in targets:
-        @pl.when(target_of(d, k) != j)
-        def _():
-            scatter(d, k).wait_send()
-            scatter_stats(d, k).wait_send()
-
     @pl.when(c == 0)
     def _():
         lend.wait_send()
+        lend_stats().wait_send()
+        for n in range(chunks):
+            give(n, i).wait_send()
 
     @pl.when(c == CORES - 1)
     def _():
+        for n in range(chunks):
+            for d, k in targets:
+                @pl.when(target_of(d, k, n) != j)
+                def _():
+                    scatter(d, k, n).wait_send()
+                    scatter_stats(d, k, n).wait_send()
         for y in vy_peers:
             remote(o3.at[y], in3.at[a], s3_r, i, y).wait_send()
 
@@ -447,19 +466,19 @@
             vmem((1, var_slot.shape[0]), jnp.int32),
             vmem((held, width), BF16),
             vmem((ny, rows, lane), BF16),
-            vmem((rows, lane), BF16),
+            vmem((CORES, rows, lane), BF16),
             vmem((CORES, 2, lheads, rows), BF16),
             vmem((ny, 2, lheads, rows), BF16),
             vmem((2 * lheads, width), BF16),
             vmem((held, lheads), BF16),
-            vmem((nx, CORES, lheads, group), F32),
-            vmem((nx * CORES, lheads, group), F32),
-            vmem((CORES, lheads, group), F32),
+            vmem((nx, 2 * lheads, group), F32),
+            vmem((nx * CORES, 2 * lheads, group), F32),
+            vmem((CORES, chunks, lheads, group), F32),
             vmem((na, lheads, group), F32),
-            vmem((nx, group, lane), F32),
+            vmem((nx * CORES, group, lane), F32),
             vmem((chunks, nx, group, lane // chunks), BF16),
-            vmem((nx * CORES, group, lane // chunks), BF16),
-            vmem((na // CORES, group, CORES * rows), BF16),
+            vmem((chunks, nx * CORES, group, lane // chunks), BF16),
+            vmem((chunks, na // CORES, group, CORES * rows), BF16),
             vmem((na, group, CORES * rows), BF16),
             vmem((ny, own, width), BF16),
             vmem((na, own, width), BF16),
@@ -467,8 +486,8 @@
             vmem((held, lane), F32),
             vmem((patches, 128), F32),
             vmem((na, group, CORES * rows), F32),
-            dma((10,)), dma, dma, dma((chunks, na)), dma((chunks, na)), dma, dma, dma, dma,
-            dma, dma, dma,
+            dma((12,)), dma, dma, dma((chunks, na)), dma((chunks, na)), dma, dma, dma, dma,
+            dma((chunks,)), dma, dma,
         ],
         compiler_params=pltpu.CompilerParams(
             collective_id=0, has_side_effects=True, vmem_limit_bytes=56 * 1024 * 1024),

time: 28.6 us -> 27.5 us (0.962)
  Pallas kernels: 27.8 us -> 26.5 us
    pallas_call x1, Pallas kernels: 27.8 us -> 26.5 us  [shards(): pl.pallas_call(functools.partial(kernel, nx, ny, heads), out_shape=vmem((...]
where the time goes in v5:
time: 27.5 us; the launch traced here: 27.1 us
  Pallas kernels  26.5 us (96%)
  local copies, waits for them, and re-layouts  0.61 us (2%)
    pallas_call x1, Pallas kernels, shards(): pl.pallas_call(functools.partial(kernel, nx, ny, heads), out_shape=vmem((...  26.5 us
    unnamed x1, local copies, waits for them, and re-layouts  0.61 us

profile of v5, /device:TPU:0, one launch (start us, length us, event | category | flops | bytes accessed | tf_op | source)
XLA Modules:
  0.0 27.1 jit_solution(8409096834320579060)
XLA Ops:
  0.0 26.5 %shard_map.73 = bf16[8,1024]{1,0:T(8,128)(2,1)S(1)} custom-call(bf16[3,256,1024]{2,1,0:T(8,128)(2,1)} %bitcast.4, bf16[91,1024]{1,0:T(8,128)(2,1)} %emb_any.1, bf16[1024]{0:T(1024)(128)(2,1)} %qry_any.1, bf16[128,1024]{1,0:T(8,128)(2,1)} %wk_any.1, bf16[128,1024]{1,0:T(8,128)(2,1)} %wv_any.1, bf16[128,1024]{1,0:T(8,128)(2,1)} %wo_any.1, s32[1,91]{1,0:T(1,128)} %bitcast.5), custom_call_target="tpu_custom_call" | custom-call | tf_op jit(solution)/shard_map/pallas_call | solution.py:455
  26.5 0.6 %copy.9 = bf16[1,8,1024]{2,1,0:T(8,128)(2,1)} copy(bf16[1,8,1024]{2,1,0:T(8,128)(2,1)S(1)} %bitcast.3) | data formatting | bytes 32768

commit v6 on v5

--- a/solution.py
+++ b/solution.py
@@ -370,12 +370,7 @@
     spot = lax.rem(a, half_planes)
     my_chunk = 1 - block // CORES
     my_lane = lax.rem(block, CORES)
-    side = a // first_plane
-    fold = a + side * (na - 1 - 2 * a)
-    steps = [na - 1 - k - (k + fold + 1) // na for k in range(na - 1)]
-    far_first = [p + side * (na - 1 - 2 * p) for p in steps]
-    turned = (1 - side) * ((a + na - 1) // na)
-    root_first = [far_first[k] + turned * (far_first[k - 1] - far_first[k]) for k in range(na - 1)]
+    root_first = [k + (k + na - a) // na for k in range(na - 1)]
 
     @pl.when(c == CORES - 1)
     def _():

time: 27.5 us -> 27.4 us (level)
  no operation moved by 1% of the time
where the time goes in v6:
time: 27.4 us; the launch traced here: 27.1 us
  Pallas kernels  26.5 us (97%)
  local copies, waits for them, and re-layouts  0.61 us (2%)
    pallas_call x1, Pallas kernels, shards(): pl.pallas_call(functools.partial(kernel, nx, ny, heads), out_shape=vmem((...  26.5 us
    unnamed x1, local copies, waits for them, and re-layouts  0.61 us

profile of v6, /device:TPU:0, one launch (start us, length us, event | category | flops | bytes accessed | tf_op | source)
XLA Modules:
  0.0 27.1 jit_solution(4506734899540879059)
XLA Ops:
  0.0 26.5 %shard_map.73 = bf16[8,1024]{1,0:T(8,128)(2,1)S(1)} custom-call(bf16[3,256,1024]{2,1,0:T(8,128)(2,1)} %bitcast.4, bf16[91,1024]{1,0:T(8,128)(2,1)} %emb_any.1, bf16[1024]{0:T(1024)(128)(2,1)} %qry_any.1, bf16[128,1024]{1,0:T(8,128)(2,1)} %wk_any.1, bf16[128,1024]{1,0:T(8,128)(2,1)} %wv_any.1, bf16[128,1024]{1,0:T(8,128)(2,1)} %wo_any.1, s32[1,91]{1,0:T(1,128)} %bitcast.5), custom_call_target="tpu_custom_call" | custom-call | tf_op jit(solution)/shard_map/pallas_call | solution.py:450
  26.5 0.6 %copy.9 = bf16[1,8,1024]{2,1,0:T(8,128)(2,1)} copy(bf16[1,8,1024]{2,1,0:T(8,128)(2,1)S(1)} %bitcast.3) | data formatting | bytes 32768

commit v7 on v6

--- a/solution.py
+++ b/solution.py
@@ -141,7 +141,7 @@
     for n in range(chunks):
         for x in a_peers:
             along_z(i, n, x, z_r.at[n, a])
-            if n == 0 and x is a_peers[0]:
+            if n == 0 and x is a_peers[-1]:
                 for y in vy_peers:
                     send(kq_mine.at[y % CORES], kq_in.at[j], kq_r, i, y)
         if n == 0:
@@ -159,7 +159,7 @@
     def share(n, x):
         here = pair_rows(x, i, n)
         arrived(here, z_r.at[n, x])
-        for q in x_peers[1:] if n > 0 or x is a_peers[0] else x_peers:
+        for q in reversed(x_peers[1:] if n > 0 or x is a_peers[0] else x_peers):
             send(here, here, w_r.at[n, x], q, j)
 
     def complete(n, sources):
@@ -308,27 +308,34 @@
     def scatter_stats(d, k, n):
         return remote(st2.at[d, n], st2_in.at[a], st2_r, i, target_of(d, k, n))
 
+    def below_of(d):
+        tops = [st_in[q * CORES + d, 0:lheads] for q in range(nx)]
+        high = functools.reduce(jnp.maximum, tops)
+        return high, [jnp.exp(top - high) for top in tops]
+
     def plane_stats():
         with jax.named_scope("K_st"):
             arrived(st_in.at[0:nx * CORES - 1], st_r)
         for d in range(CORES):
-            tops = [st_in[q * CORES + d, 0:lheads] for q in range(nx)]
-            high = functools.reduce(jnp.maximum, tops)
-            below = [jnp.exp(top - high) for top in tops]
+            high, below = below_of(d)
             total = sum(below[q] * st_in[q * CORES + d, lheads:2 * lheads] for q in range(nx))
             for n in range(chunks):
                 heads_n = slice(n * cheads, (n + 1) * cheads)
                 st2[d, n, 0:cheads] = high[heads_n]
                 st2[d, n, cheads:lheads] = total[heads_n]
-            for q in range(nx):
-                f_high, f_low = split(below[q])
-                fexp[q * CORES + d] = (lax.dot_general(f_high, spread, TN, preferred_element_type=F32)
-                                       + lax.dot_general(f_low, spread, TN, preferred_element_type=F32))
         for n in range(chunks):
             for d, k in targets:
                 @pl.when(target_of(d, k, n) != j)
                 def _():
                     scatter_stats(d, k, n).start()
+
+    def plane_factors():
+        for d in range(CORES):
+            _, below = below_of(d)
+            for q in range(nx):
+                f_high, f_low = split(below[q])
+                fexp[q * CORES + d] = (lax.dot_general(f_high, spread, TN, preferred_element_type=F32)
+                                       + lax.dot_general(f_low, spread, TN, preferred_element_type=F32))
 
     def combine(n):
         arrived(in1.at[n, 0:nx * CORES - 1], s1_r.at[n])
@@ -374,6 +381,7 @@
 
     @pl.when(c == CORES - 1)
     def _():
+        plane_factors()
         for n in range(chunks):
             with jax.named_scope(f"R_combine{n}"):
                 combine(n)

time: 27.4 us -> 27.3 us (level)
  no operation moved by 1% of the time
where the time goes in v7:
time: 27.3 us; the launch traced here: 27.2 us
  Pallas kernels  26.5 us (97%)
  local copies, waits for them, and re-layouts  0.61 us (2%)
    pallas_call x1, Pallas kernels, shards(): pl.pallas_call(functools.partial(kernel, nx, ny, heads), out_shape=vmem((...  26.5 us
    unnamed x1, local copies, waits for them, and re-layouts  0.61 us

profile of v7, /device:TPU:0, one launch (start us, length us, event | category | flops | bytes accessed | tf_op | source)
XLA Modules:
  0.0 27.2 jit_solution(3223792463150479130)
XLA Ops:
  0.0 26.5 %shard_map.73 = bf16[8,1024]{1,0:T(8,128)(2,1)S(1)} custom-call(bf16[3,256,1024]{2,1,0:T(8,128)(2,1)} %bitcast.4, bf16[91,1024]{1,0:T(8,128)(2,1)} %emb_any.1, bf16[1024]{0:T(1024)(128)(2,1)} %qry_any.1, bf16[128,1024]{1,0:T(8,128)(2,1)} %wk_any.1, bf16[128,1024]{1,0:T(8,128)(2,1)} %wv_any.1, bf16[128,1024]{1,0:T(8,128)(2,1)} %wo_any.1, s32[1,91]{1,0:T(1,128)} %bitcast.5), custom_call_target="tpu_custom_call" | custom-call | tf_op jit(solution)/shard_map/pallas_call | solution.py:458
  26.6 0.6 %copy.9 = bf16[1,8,1024]{2,1,0:T(8,128)(2,1)} copy(bf16[1,8,1024]{2,1,0:T(8,128)(2,1)S(1)} %bitcast.3) | data formatting | bytes 32768
